TPU v7x, 16 devices: a whole 2x2x2 slice. The times are simulated.
16 devices in a mesh: dp: 4 (over z, y), ep: 4 (over x, core).
Axes of the slice: x: 2, y: 2, z: 2, core: 2. Of those that a mesh axis runs over, the one named last changes fastest.
Arguments:
- tokens_a: bfloat16 [512, 1536], P(('dp', 'ep')), parts along dimension 0
- experts_a: int32 [512, 8], P(('dp', 'ep')), parts along dimension 0
- slots_a: int32 [512, 8], P(('dp', 'ep')), parts along dimension 0
- gates_a: bfloat16 [512, 8], P(('dp', 'ep')), parts along dimension 0
- tokens_b: bfloat16 [512, 1536], P(('dp', 'ep')), parts along dimension 0
- experts_b: int32 [512, 8], P(('dp', 'ep')), parts along dimension 0
- slots_b: int32 [512, 8], P(('dp', 'ep')), parts along dimension 0
- gates_b: bfloat16 [512, 8], P(('dp', 'ep')), parts along dimension 0
- attn_gain: bfloat16 [1536], replicated
- w_query: bfloat16 [1536, 24, 64], replicated
- w_key: bfloat16 [1536, 24, 64], replicated
- w_value: bfloat16 [1536, 24, 64], replicated
- w_out: bfloat16 [24, 64, 1536], replicated
- moe_gain: bfloat16 [1536], replicated
- w_gate: bfloat16 [40, 1536, 512], P('ep')
- w_up: bfloat16 [40, 1536, 512], P('ep')
- w_down: bfloat16 [40, 512, 1536], P('ep')
Outputs:
- output 1: bfloat16 [512, 1536], P(('dp', 'ep')), parts along dimension 0
- output 2: bfloat16 [512, 1536], P(('dp', 'ep')), parts along dimension 0
There are 4 independent parts. A program takes and returns all parts, laid end to end along the dimension named above; an argument that names none is the same for every part.
All inputs are finite; a program needn't handle non-finite values.
Results may differ from a plain program's by a relative error of at most 0.0137052.
Values are sent between devices in bfloat16 or wider.
A program may use at most 1 GiB of HBM per device.

v0:
```python
import jax
import jax.numpy as jnp
from jax import lax
from jax.sharding import PartitionSpec as P

NORM_EPS = 1e-6
MASK_VALUE = -1e30


def rms_norm(rows, gain_vec):
    rows_f = rows.astype(jnp.float32)
    inv_rms = lax.rsqrt(jnp.mean(rows_f * rows_f, axis=-1, keepdims=True) + NORM_EPS)
    return (rows_f * inv_rms * gain_vec.astype(jnp.float32)).astype(jnp.bfloat16)


def attention_block(sequence, attn_gain, w_query, w_key, w_value, w_out):
    seq_len = sequence.shape[0]
    normed = rms_norm(sequence, attn_gain)
    query = jnp.einsum("td,dhe->the", normed, w_query, preferred_element_type=jnp.float32).astype(jnp.bfloat16)
    keys = jnp.einsum("td,dhe->the", normed, w_key, preferred_element_type=jnp.float32).astype(jnp.bfloat16)
    values = jnp.einsum("td,dhe->the", normed, w_value, preferred_element_type=jnp.float32).astype(jnp.bfloat16)
    scores = jnp.einsum("qhe,khe->hqk", query, keys, preferred_element_type=jnp.float32) * (w_query.shape[2] ** -0.5)
    causal = lax.broadcasted_iota(jnp.int32, (seq_len, seq_len), 0) >= lax.broadcasted_iota(jnp.int32, (seq_len, seq_len), 1)
    scores = jnp.where(causal[None, :, :], scores, MASK_VALUE)
    attn_prob = jax.nn.softmax(scores, axis=-1).astype(jnp.bfloat16)
    context = jnp.einsum("hqk,khe->qhe", attn_prob, values, preferred_element_type=jnp.float32).astype(jnp.bfloat16)
    attn_out = jnp.einsum("qhe,hed->qd", context, w_out, preferred_element_type=jnp.float32)
    return (sequence.astype(jnp.float32) + attn_out).astype(jnp.bfloat16)


def capacity_of(seq_len, top_k, experts_total):
    return 8 * max(1, (seq_len * top_k) // (4 * experts_total))


def dispatch_rows(normed, dest_row, experts_total, capacity):
    seq_len, model_dim = normed.shape
    top_k = dest_row.shape[0] // seq_len
    token_of = jnp.arange(seq_len * top_k, dtype=jnp.int32) // top_k
    source = jnp.full((experts_total * capacity,), seq_len, jnp.int32).at[dest_row].set(token_of, mode="drop")
    return jnp.take(normed, source, axis=0, mode="fill", fill_value=0).reshape(experts_total, capacity, model_dim)


def combine_rows(residual, returned, dest_row, gates):
    seq_len, model_dim = residual.shape
    top_k = gates.shape[1]
    picked = jnp.take(returned.reshape(-1, model_dim), dest_row, axis=0, mode="fill", fill_value=0).reshape(seq_len, top_k, model_dim)
    mixed_sum = jnp.einsum("tk,tkd->td", gates, picked, preferred_element_type=jnp.float32)
    return (residual.astype(jnp.float32) + mixed_sum).astype(jnp.bfloat16)


def expert_ffn(received, w_gate, w_up, w_down):
    gate_act = jnp.einsum("pecd,edf->pecf", received, w_gate, preferred_element_type=jnp.float32)
    up_act = jnp.einsum("pecd,edf->pecf", received, w_up, preferred_element_type=jnp.float32)
    hidden = (jax.nn.silu(gate_act) * up_act).astype(jnp.bfloat16)
    return jnp.einsum("pecf,efd->pecd", hidden, w_down, preferred_element_type=jnp.float32).astype(jnp.bfloat16)


def moe_layer(tokens, experts, slots, gates, attn_gain, w_query, w_key, w_value, w_out, moe_gain, w_gate, w_up, w_down, group):
    seq_len, model_dim = tokens.shape
    local_experts = w_gate.shape[0]
    experts_total = local_experts * group
    capacity = capacity_of(seq_len, experts.shape[1], experts_total)
    residual = attention_block(tokens, attn_gain, w_query, w_key, w_value, w_out)
    normed = rms_norm(residual, moe_gain)
    dest_row = jnp.where(slots >= 0, experts * capacity + slots, experts_total * capacity).reshape(-1)
    dispatched = dispatch_rows(normed, dest_row, experts_total, capacity)
    received = lax.all_to_all(dispatched, "ep", 0, 0, tiled=True).reshape(group, local_experts, capacity, model_dim)
    expert_out = expert_ffn(received, w_gate, w_up, w_down).reshape(experts_total, capacity, model_dim)
    returned = lax.all_to_all(expert_out, "ep", 0, 0, tiled=True)
    return combine_rows(residual, returned, dest_row, gates)


def solution(mesh):
    group = mesh.shape["ep"]
    row_spec = P(("dp", "ep"), None)
    full_spec = P(None, None, None)
    gain_spec = P(None)
    expert_spec = P("ep", None, None)
    in_specs = (row_spec, row_spec, row_spec, row_spec, row_spec, row_spec, row_spec, row_spec, gain_spec, full_spec, full_spec, full_spec, full_spec, gain_spec, expert_spec, expert_spec, expert_spec)

    def device_fn(tokens_a, experts_a, slots_a, gates_a, tokens_b, experts_b, slots_b, gates_b, attn_gain, w_query, w_key, w_value, w_out, moe_gain, w_gate, w_up, w_down):
        out_a = moe_layer(tokens_a, experts_a, slots_a, gates_a, attn_gain, w_query, w_key, w_value, w_out, moe_gain, w_gate, w_up, w_down, group)
        out_b = moe_layer(tokens_b, experts_b, slots_b, gates_b, attn_gain, w_query, w_key, w_value, w_out, moe_gain, w_gate, w_up, w_down, group)
        return out_a, out_b

    return jax.shard_map(device_fn, mesh=mesh, in_specs=in_specs, out_specs=(row_spec, row_spec), check_vma=False)
```

profile of v0, /device:TPU:0, one launch (start us, length us, event | category | flops | bytes accessed | tf_op | source)
XLA Modules:
  0.0 132.5 jit_solution(7309532544532861552)
XLA Ops:
  0.6 0.0 copy-start.1
  0.6 0.0 copy-start
  0.7 0.0 slice-start
  0.7 0.8 convert_element_type.103
  1.5 1.5 %fusion.99 = f32[32]{0:T(128)S(1)} fusion(bf16[32,1536]{1,0:T(8,128)(2,1)} %param.25), kind=kLoop, calls=%fused_computation.93 | loop fusion | flops 147424 | bytes 98432 | tf_op jit(solution)/shard_map/reduce_sum | solution.py:12
  3.0 0.0 copy-start.2
  3.0 0.0 slice-start.1
  3.0 5.0 %convolution_convert_fusion.2 = bf16[32,24,64]{2,0,1:T(8,128)(2,1)S(1)} fusion(bf16[1536,24,64]{0,2,1:T(8,128)(2,1)} %param.31, bf16[32,1536]{1,0:T(8,128)(2,1)} %param.25, f32[32]{0:T(128)S(1)} %add_rsqrt_fusion.1, f32[1536]{0:T(1024)S(1)} %convert_element_type.103), kind=kOutput, calls=%fused_computation.50 | convolution fusion | flops 151240704 | bytes 4921472 | tf_op jit(solution)/shard_map/td,dhe->the/dot_general | solution.py:20
  8.0 0.0 copy-done.1
  8.0 0.0 copy-done
  8.1 2.2 %fusion.134 = bf16[32,24,64]{2,0,1:T(8,128)(2,1)S(1)} fusion(bf16[1536,24,64]{0,2,1:T(8,128)(2,1)S(1)} %copy-done, bf16[32,1536]{1,0:T(8,128)(2,1)S(1)} %copy-done.1, f32[32]{0:T(128)S(1)} %add_rsqrt_fusion.1, f32[1536]{0:T(1024)S(1)} %convert_element_type.103), kind=kOutput, calls=%fused_computation.146 | convolution fusion | flops 151191552 | bytes 4921472 | tf_op jit(solution)/shard_map/td,dhe->the/dot_general | solution.py:21
  10.3 0.0 copy-done.2
  10.3 0.1 fusion.96
  10.5 0.0 slice-done
  10.5 0.0 copy-start.3
  10.5 0.0 copy-start.4
  10.5 2.2 %convolution_convert_fusion.4 = bf16[32,24,64]{2,0,1:T(8,128)(2,1)S(1)} fusion(bf16[1536,24,64]{0,2,1:T(8,128)(2,1)S(1)} %bitcast.160, bf16[32,1536]{1,0:T(8,128)(2,1)S(1)} %copy-done.2, f32[1536]{0:T(1024)S(1)} %convert_element_type.103, f32[32]{0:T(128)S(1)} %add_rsqrt_fusion.3), kind=kOutput, calls=%fused_computation.52 | convolution fusion | flops 151240704 | bytes 4921472 | tf_op jit(solution)/shard_map/td,dhe->the/dot_general | solution.py:20
  12.8 2.2 %fusion.129 = bf16[32,24,64]{2,0,1:T(8,128)(2,1)S(1)} fusion(bf16[1536,24,64]{0,2,1:T(8,128)(2,1)S(1)} %copy-done, bf16[32,1536]{1,0:T(8,128)(2,1)S(1)} %copy-done.2, f32[1536]{0:T(1024)S(1)} %convert_element_type.103, f32[32]{0:T(128)S(1)} %add_rsqrt_fusion.3), kind=kOutput, calls=%fused_computation.145 | convolution fusion | flops 151191552 | bytes 4921472 | tf_op jit(solution)/shard_map/td,dhe->the/dot_general | solution.py:21
  15.1 0.1 copy.23
  15.1 0.1 reshape.162
  15.2 1.4 %scatter_custom_fusion.1 = s32[320]{0:T(512)S(1)} fusion(s32[256]{0:T(256)S(1)} %bitcast.170, s32[256]{0:T(256)S(1)} %and_select_fusion, s32[]{:T(128)} %constant.61.clone.1), kind=kCustom, calls=%fused_computation.131 | custom fusion | bytes 1284 | tf_op jit(solution)/shard_map/scatter | solution.py:39
  16.7 4.7 %fusion.61 = f32[24,32,32]{1,2,0:T(8,128)S(1)} fusion(bf16[32,24,64]{2,0,1:T(8,128)(2,1)S(1)} %convolution_convert_fusion.2, bf16[1536,24,64]{0,2,1:T(8,128)(2,1)} %param.30, pred[32,32]{0,1:T(8,128)(4,1)S(1)} %iota_compare_fusion, bf16[32,1536]{1,0:T(8,128)(2,1)S(1)} %copy-done.1, f32[32]{0:T(128)S(1)} %add_rsqrt_fusion.1, f32[1536]{0:T(1024)S(1)} %convert_element_type.103), kind=kOutput, calls=%fused_computation.47 | convolution fusion | flops 154435584 | bytes 5020800 | tf_op jit(solution)/shard_map/qhe,khe->hqk/dot_general | solution.py:22
  21.4 0.1 fusion.137
  21.5 0.1 copy.60
  21.6 4.7 %fusion.60 = f32[24,32,32]{1,2,0:T(8,128)S(1)} fusion(bf16[32,24,64]{2,0,1:T(8,128)(2,1)S(1)} %convolution_convert_fusion.4, bf16[1536,24,64]{0,2,1:T(8,128)(2,1)} %param.30, pred[32,32]{0,1:T(8,128)(4,1)S(1)} %iota_compare_fusion, bf16[32,1536]{1,0:T(8,128)(2,1)S(1)} %copy-done.2, f32[1536]{0:T(1024)S(1)} %convert_element_type.103, f32[32]{0:T(128)S(1)} %add_rsqrt_fusion.3), kind=kOutput, calls=%fused_computation.46 | convolution fusion | flops 154435584 | bytes 5020800 | tf_op jit(solution)/shard_map/qhe,khe->hqk/dot_general | solution.py:22
  26.3 0.1 fusion.136
  26.5 0.1 copy.61
  26.5 0.0 copy-done.5
  26.6 3.6 %multiply_reduce_fusion = (f32[32]{0:T(128)S(1)}, f32[32,1536]{1,0:T(8,128)S(1)}) fusion(bf16[24,64,1536]{2,1,0:T(8,128)(2,1)} %param.33, bf16[32,24,64]{2,1,0:T(8,128)(2,1)S(1)} %copy.60, f32[24,32]{1,0:T(8,128)S(1)} %fusion.137, f32[24,32,32]{1,2,0:T(8,128)S(1)} %fusion.61, bf16[32,1536]{1,0:T(8,128)(2,1)S(1)} %copy-done.1), kind=kOutput, calls=%fused_computation.103 | convolution fusion | flops 154559232 | bytes 5213312 | tf_op jit(solution)/shard_map/qhe,hed->qd/dot_general | solution.py:27
  30.2 3.6 %multiply_reduce_fusion.1 = (f32[32]{0:T(128)S(1)}, f32[32,1536]{1,0:T(8,128)S(1)}) fusion(bf16[24,64,1536]{2,1,0:T(8,128)(2,1)} %param.33, bf16[32,24,64]{2,1,0:T(8,128)(2,1)S(1)} %copy.61, f32[24,32]{1,0:T(8,128)S(1)} %fusion.136, f32[24,32,32]{1,2,0:T(8,128)S(1)} %fusion.60, bf16[32,1536]{1,0:T(8,128)(2,1)S(1)} %copy-done.2), kind=kOutput, calls=%fused_computation.106 | convolution fusion | flops 154559232 | bytes 5213312 | tf_op jit(solution)/shard_map/qhe,hed->qd/dot_general | solution.py:27
  33.9 0.1 multiply_convert_fusion
  34.0 0.0 copy-start.6
  34.0 0.0 copy-start.7
  34.0 2.2 %gather_fusion.2 = bf16[320,1536]{1,0:T(8,128)(2,1)S(1)} fusion(bf16[32,1536]{1,0:T(8,128)(2,1)S(1)} %get-tuple-element.4, s32[1024]{0:T(1024)S(1)} %pad_clamp_fusion.1), kind=kCustom, calls=%fused_computation.2.clone | custom fusion | bytes 1967360 | tf_op jit(solution)/shard_map/jit(_take)/gather | solution.py:40
  36.2 1.1 select_bitcast_fusion
  37.4 4.5 %all-to-all-start.2 = ((bf16[40,8,1536]{2,1,0:T(8,128)(2,1)}), bf16[40,8,1536]{2,1,0:T(8,128)(2,1)S(1)}, u32[]{:S(2)}, u32[]{:S(2)}) async-start(bf16[40,8,1536]{2,1,0:T(8,128)(2,1)} %select_bitcast_fusion), calls=%async_computation.2 | async-start | bytes 1966080 | tf_op jit(solution)/shard_map/all_to_all | solution.py:67
  41.9 0.1 reshape.167
  42.0 0.1 copy.19
  42.1 0.1 reshape.155
  42.2 1.4 %scatter_custom_fusion = s32[320]{0:T(512)S(1)} fusion(s32[256]{0:T(256)S(1)} %bitcast.169, s32[256]{0:T(256)S(1)} %and_select_fusion, s32[]{:T(128)} %constant.61.clone.1), kind=kCustom, calls=%fused_computation.133 | custom fusion | bytes 1284 | tf_op jit(solution)/shard_map/scatter | solution.py:39
  43.6 0.1 reshape.160
  43.7 2.2 %gather_fusion = bf16[320,1536]{1,0:T(8,128)(2,1)S(1)} fusion(bf16[32,1536]{1,0:T(8,128)(2,1)S(1)} %get-tuple-element.5, s32[1024]{0:T(1024)S(1)} %pad_clamp_fusion.3), kind=kCustom, calls=%fused_computation.clone | custom fusion | bytes 1967360 | tf_op jit(solution)/shard_map/jit(_take)/gather | solution.py:40
  46.0 1.1 select_bitcast_fusion.1
  47.1 8.4 %all-to-all-done.2 = bf16[40,8,1536]{2,1,0:T(8,128)(2,1)S(1)} async-done(((bf16[40,8,1536]{2,1,0:T(8,128)(2,1)}), bf16[40,8,1536]{2,1,0:T(8,128)(2,1)S(1)}, u32[]{:S(2)}, u32[]{:S(2)}) %all-to-all-start.2) | async-done | bytes 983072 | tf_op jit(solution)/shard_map/all_to_all | solution.py:67
  55.5 3.5 %all-to-all-start = ((bf16[40,8,1536]{2,1,0:T(8,128)(2,1)}), bf16[40,8,1536]{2,1,0:T(8,128)(2,1)S(1)}, u32[]{:S(2)}, u32[]{:S(2)}) async-start(bf16[40,8,1536]{2,1,0:T(8,128)(2,1)} %select_bitcast_fusion.1), calls=%async_computation | async-start | bytes 1966080 | tf_op jit(solution)/shard_map/all_to_all | solution.py:67
  59.0 9.0 %fusion.35 = f32[4,10,8,512]{3,2,0,1:T(8,128)} fusion(bf16[10,1536,512]{2,1,0:T(8,128)(2,1)} %param.35, bf16[4,10,8,1536]{3,2,1,0:T(8,128)(2,1)S(1)} %bitcast.161), kind=kOutput, calls=%fused_computation.33 | convolution fusion | flops 503316480 | bytes 17367040 | tf_op jit(solution)/shard_map/pecd,edf->pecf/dot_general | solution.py:52
  68.0 15.1 %fusion.20 = bf16[4,10,8,1536]{3,2,0,1:T(8,128)(2,1)S(1)} fusion(bf16[10,512,1536]{2,1,0:T(8,128)(2,1)} %param.37, bf16[10,1536,512]{2,1,0:T(8,128)(2,1)} %param.36, bf16[4,10,8,1536]{3,2,1,0:T(8,128)(2,1)S(1)} %bitcast.162, f32[4,10,8,512]{3,2,0,1:T(8,128)} %fusion.35), kind=kOutput, calls=%fused_computation.22 | convolution fusion | flops 1008107520 | bytes 34078720 | tf_op jit(solution)/shard_map/pecf,efd->pecd/dot_general | solution.py:55
  83.1 1.1 copy.26
  84.2 0.0 all-to-all-done
  84.2 3.7 %all-to-all-start.3 = ((bf16[40,8,1536]{2,1,0:T(8,128)(2,1)}), bf16[40,8,1536]{2,1,0:T(8,128)(2,1)S(1)}, u32[]{:S(2)}, u32[]{:S(2)}) async-start(bf16[40,8,1536]{2,1,0:T(8,128)(2,1)} %bitcast.166), calls=%async_computation.3 | async-start | bytes 1966080 | tf_op jit(solution)/shard_map/all_to_all | solution.py:69
  87.9 9.0 %fusion.32 = f32[4,10,8,512]{3,2,0,1:T(8,128)} fusion(bf16[10,1536,512]{2,1,0:T(8,128)(2,1)} %param.35, bf16[4,10,8,1536]{3,2,1,0:T(8,128)(2,1)S(1)} %bitcast.163), kind=kOutput, calls=%fused_computation.32 | convolution fusion | flops 503316480 | bytes 17367040 | tf_op jit(solution)/shard_map/pecd,edf->pecf/dot_general | solution.py:52
  96.9 15.2 %fusion.23 = bf16[4,10,8,1536]{3,2,0,1:T(8,128)(2,1)S(1)} fusion(bf16[10,512,1536]{2,1,0:T(8,128)(2,1)} %param.37, bf16[10,1536,512]{2,1,0:T(8,128)(2,1)} %param.36, bf16[4,10,8,1536]{3,2,1,0:T(8,128)(2,1)S(1)} %bitcast.164, f32[4,10,8,512]{3,2,0,1:T(8,128)} %fusion.32), kind=kOutput, calls=%fused_computation.23 | convolution fusion | flops 1008107520 | bytes 34078720 | tf_op jit(solution)/shard_map/pecf,efd->pecd/dot_general | solution.py:55
  112.1 1.0 copy.22
  113.1 0.0 all-to-all-done.3
  113.1 3.5 %all-to-all-start.1 = ((bf16[40,8,1536]{2,1,0:T(8,128)(2,1)}), bf16[40,8,1536]{2,1,0:T(8,128)(2,1)S(1)}, u32[]{:S(2)}, u32[]{:S(2)}) async-start(bf16[40,8,1536]{2,1,0:T(8,128)(2,1)} %bitcast.165), calls=%async_computation.1 | async-start | bytes 1966080 | tf_op jit(solution)/shard_map/all_to_all | solution.py:69
  116.7 0.1 copy.36
  116.8 0.1 copy.32
  116.8 1.3 gather_fusion.3
  118.1 0.4 fusion.68
  118.5 0.7 fusion.102
  119.2 10.9 %all-to-all-done.1 = bf16[40,8,1536]{2,1,0:T(8,128)(2,1)S(1)} async-done(((bf16[40,8,1536]{2,1,0:T(8,128)(2,1)}), bf16[40,8,1536]{2,1,0:T(8,128)(2,1)S(1)}, u32[]{:S(2)}, u32[]{:S(2)}) %all-to-all-start.1) | async-done | bytes 983072 | tf_op jit(solution)/shard_map/all_to_all | solution.py:69
  130.1 1.3 gather_fusion.1
  131.4 0.4 fusion.70
  131.8 0.7 fusion.103
  (33 shorter events, 0.2 us)
Async XLA Ops:
  0.6 7.4 %copy-start.1 = (bf16[32,1536]{1,0:T(8,128)(2,1)S(1)}, bf16[32,1536]{1,0:T(8,128)(2,1)}, u32[]{:S(2)}) copy-start(bf16[32,1536]{1,0:T(8,128)(2,1)} %param.25) | copy-start | bytes 294916
  0.6 7.4 %copy-start = (bf16[1536,24,64]{0,2,1:T(8,128)(2,1)S(1)}, bf16[1536,24,64]{0,2,1:T(8,128)(2,1)}, u32[]{:S(2)}) copy-start(bf16[1536,24,64]{0,2,1:T(8,128)(2,1)} %param.32) | copy-start | bytes 14155780
  0.7 9.8 %slice-start = ((s8[4718592]{0:T(1024)(128)(4,1)}), s8[4194304]{0:T(1024)(128)(4,1)S(1)}, s32[]{:S(2)}) async-start(s8[4718592]{0:T(1024)(128)(4,1)} %bitcast.159), calls=%async_computation.4 | async-start | bytes 8388608
  3.0 7.3 %copy-start.2 = (bf16[32,1536]{1,0:T(8,128)(2,1)S(1)}, bf16[32,1536]{1,0:T(8,128)(2,1)}, u32[]{:S(2)}) copy-start(bf16[32,1536]{1,0:T(8,128)(2,1)} %param.21) | copy-start | bytes 294916
  3.0 7.4 %slice-start.1 = ((s8[4718592]{0:T(1024)(128)(4,1)}), s8[524288]{0:T(1024)(128)(4,1)S(1)}, s32[]{:S(2)}) async-start(s8[4718592]{0:T(1024)(128)(4,1)} %bitcast.159), calls=%async_computation.5 | async-start | bytes 1048576
  10.5 4.5 %copy-start.3 = (s32[32,8]{0,1:T(8,128)S(1)}, s32[32,8]{0,1:T(8,128)}, u32[]{:S(2)}) copy-start(s32[32,8]{0,1:T(8,128)} %param.27) | copy-start | bytes 3076
  10.5 4.5 %copy-start.4 = (s32[32,8]{0,1:T(8,128)S(1)}, s32[32,8]{0,1:T(8,128)}, u32[]{:S(2)}) copy-start(s32[32,8]{0,1:T(8,128)} %param.26) | copy-start | bytes 3076
  21.4 5.2 %copy-start.5 = (bf16[1536]{0:T(1024)(128)(2,1)S(1)}, bf16[1536]{0:T(1024)(128)(2,1)}, u32[]{:S(2)}) copy-start(bf16[1536]{0:T(1024)(128)(2,1)} %param.34) | copy-start | bytes 9220
  34.0 8.0 %copy-start.6 = (s32[32,8]{0,1:T(8,128)S(1)}, s32[32,8]{0,1:T(8,128)}, u32[]{:S(2)}) copy-start(s32[32,8]{0,1:T(8,128)} %param.23) | copy-start | bytes 3076
  34.0 8.0 %copy-start.7 = (s32[32,8]{0,1:T(8,128)S(1)}, s32[32,8]{0,1:T(8,128)}, u32[]{:S(2)}) copy-start(s32[32,8]{0,1:T(8,128)} %param.22) | copy-start | bytes 3076
  37.4 18.1 %all-to-all-start.2 = ((bf16[40,8,1536]{2,1,0:T(8,128)(2,1)}), bf16[40,8,1536]{2,1,0:T(8,128)(2,1)S(1)}, u32[]{:S(2)}, u32[]{:S(2)}) async-start(bf16[40,8,1536]{2,1,0:T(8,128)(2,1)} %select_bitcast_fusion), calls=%async_computation.2 | async-start | bytes 1966080 | tf_op jit(solution)/shard_map/all_to_all | solution.py:67
  55.5 28.7 %all-to-all-start = ((bf16[40,8,1536]{2,1,0:T(8,128)(2,1)}), bf16[40,8,1536]{2,1,0:T(8,128)(2,1)S(1)}, u32[]{:S(2)}, u32[]{:S(2)}) async-start(bf16[40,8,1536]{2,1,0:T(8,128)(2,1)} %select_bitcast_fusion.1), calls=%async_computation | async-start | bytes 1966080 | tf_op jit(solution)/shard_map/all_to_all | solution.py:67
  84.2 28.9 %all-to-all-start.3 = ((bf16[40,8,1536]{2,1,0:T(8,128)(2,1)}), bf16[40,8,1536]{2,1,0:T(8,128)(2,1)S(1)}, u32[]{:S(2)}, u32[]{:S(2)}) async-start(bf16[40,8,1536]{2,1,0:T(8,128)(2,1)} %bitcast.166), calls=%async_computation.3 | async-start | bytes 1966080 | tf_op jit(solution)/shard_map/all_to_all | solution.py:69
  96.9 19.8 %copy-start.8 = (bf16[32,8]{0,1:T(8,128)(2,1)S(1)}, bf16[32,8]{0,1:T(8,128)(2,1)}, u32[]{:S(2)}) copy-start(bf16[32,8]{0,1:T(8,128)(2,1)} %param.28) | copy-start | bytes 1540
  96.9 19.9 %copy-start.9 = (bf16[32,8]{0,1:T(8,128)(2,1)S(1)}, bf16[32,8]{0,1:T(8,128)(2,1)}, u32[]{:S(2)}) copy-start(bf16[32,8]{0,1:T(8,128)(2,1)} %param.24) | copy-start | bytes 1540
  113.1 17.0 %all-to-all-start.1 = ((bf16[40,8,1536]{2,1,0:T(8,128)(2,1)}), bf16[40,8,1536]{2,1,0:T(8,128)(2,1)S(1)}, u32[]{:S(2)}, u32[]{:S(2)}) async-start(bf16[40,8,1536]{2,1,0:T(8,128)(2,1)} %bitcast.165), calls=%async_computation.1 | async-start | bytes 1966080 | tf_op jit(solution)/shard_map/all_to_all | solution.py:69
where the time goes:
time: 133 us; the launch traced here: 132 us
  matrix products  77.5 us (58%)
  waiting for transfers between devices  19.3 us (15%)
  starting transfers between devices  15.3 us (12%)
  local copies, waits for them, and re-layouts  12.8 us (10%)
  other arithmetic  6.49 us (5%)
    dot_general x2, matrix products, expert_ffn(): jnp.einsum('pecf,efd->pecd', hidden, w_down, preferred_element_type=jnp.f...  30.3 us
    dot_general x2, matrix products, expert_ffn(): jnp.einsum('pecd,edf->pecf', received, w_gate, preferred_element_type=jnp...  18 us
    all_to_all x2, waiting for transfers between devices, moe_layer(): returned = lax.all_to_all(expert_out, 'ep', 0, 0, tiled=True)  10.9 us
    dot_general x2, matrix products, attention_block(): jnp.einsum('qhe,khe->hqk', query, keys, preferred_element_type=jnp.float32)  9.44 us
    all_to_all x2, waiting for transfers between devices, moe_layer(): lax.all_to_all(dispatched, 'ep', 0, 0, tiled=True)  8.39 us
    all_to_all x2, starting transfers between devices, moe_layer(): lax.all_to_all(dispatched, 'ep', 0, 0, tiled=True)  8.01 us
    dot_general x2, matrix products, attention_block(): jnp.einsum('qhe,hed->qd', context, w_out, preferred_element_type=jnp.floa...  7.26 us
    all_to_all x2, starting transfers between devices, moe_layer(): returned = lax.all_to_all(expert_out, 'ep', 0, 0, tiled=True)  7.24 us
  transfers between devices with their start and end apart: 4, of which 2 were waited for; matrix products, arithmetic and copies ran while one was open for 44% of the time, Pallas kernels for 0%

commit v1 on v0

v1 whole, which is shorter than its diff:
```python
import functools

import jax
import jax.numpy as jnp
from jax import lax
from jax.experimental import pallas as pl
from jax.experimental.pallas import tpu as pltpu
from jax.sharding import PartitionSpec as P

NORM_EPS = 1e-6
MASK_VALUE = -1e30
MESH = pl.DeviceIdType.MESH

SEQ = 32
ROWS = 2 * SEQ
TOP_K = 8
DIM = 1536
HEAD = 64
FFN = 512
SLOTS = 8
LOCAL = 10
EXPERTS = 40
GROUP = 4
TOKENS = GROUP * ROWS
EROWS = GROUP * 2 * SLOTS
XROWS = LOCAL * EROWS
NB = 256
NBLK = DIM // NB
QCH = 512
NQ = 3 * DIM // QCH
NO = DIM // QCH

NT = (((1,), (1,)), ((), ()))
NN = (((1,), (0,)), ((), ()))


def dot(lhs, rhs, dims=NN):
    return lax.dot_general(lhs, rhs, dims, preferred_element_type=jnp.float32)


def rms_norm(rows_f, gain):
    inv_rms = lax.rsqrt(jnp.mean(rows_f * rows_f, axis=-1, keepdims=True) + NORM_EPS)
    return (rows_f * inv_rms * gain).astype(jnp.bfloat16)


def layer_kernel(
    tok_a, exp_a, slot_a, gate_a, tok_b, exp_b, slot_b, gate_b, again_h, mgain_h, wq, wk, wv, wo, wg, wu, wd,
    out_a, out_b,
    x_v, exp_v, slot_v, gate_v, again, mgain, buf1, wo_v, wg_v, wu_v, qkv, ctx, resid, u_all, codes, gts, disp, comb, xg, hid, o_v,
    p_send, p_recv, s_send, r_recv, keep, out_v,
    in_sem, q_sem, o_sem, g_sem, d_sem, out_sem, c_send, c_recv, u_send, u_recv, ps_sem, pr_sem, ss_sem, rr_sem,
):
    me = lax.axis_index("ep")
    dp = lax.axis_index("dp")
    x_pos = me // 2
    core = lax.rem(me, 2)
    sib = (dp, x_pos * 2 + (1 - core))
    cross = (dp, (1 - x_pos) * 2 + core)

    ins = []
    for i, (src, dst) in enumerate([
        (tok_a, x_v.at[pl.ds(0, SEQ)]), (tok_b, x_v.at[pl.ds(SEQ, SEQ)]), (again_h, again),
        (exp_a, exp_v.at[0]), (exp_b, exp_v.at[1]), (slot_a, slot_v.at[0]), (slot_b, slot_v.at[1]),
        (gate_a, gate_v.at[0]), (gate_b, gate_v.at[1]), (mgain_h, mgain),
    ]):
        cp = pltpu.make_async_copy(src, dst, in_sem.at[i])
        cp.start()
        ins.append(cp)

    q_cp = []
    for i in range(NQ):
        w, r = [(wq, 0), (wk, 1), (wv, 2)][i // (DIM // QCH)][0], i % (DIM // QCH)
        cp = pltpu.make_async_copy(w.at[pl.ds(r * QCH, QCH)], buf1.at[pl.ds(i * QCH, QCH)], q_sem.at[i])
        cp.start(priority=1)
        q_cp.append(cp)
    o_cp = []
    for i in range(NO):
        cp = pltpu.make_async_copy(wo.at[pl.ds(i * QCH, QCH)], wo_v.at[pl.ds(i * QCH, QCH)], o_sem.at[i])
        cp.start(priority=1)
        o_cp.append(cp)
    for e in range(LOCAL):
        pltpu.make_async_copy(wg.at[e], wg_v.at[e], g_sem.at[0, e]).start(priority=1)
        pltpu.make_async_copy(wu.at[e], wu_v.at[e], g_sem.at[1, e]).start(priority=1)

    barrier = pltpu.get_barrier_semaphore()
    for peer in (sib, cross):
        pl.semaphore_signal(barrier, inc=1, device_id=peer, device_id_type=MESH)

    for cp in ins:
        cp.wait()

    for b in range(2):
        s = slot_v[b]
        codes[0, b] = jnp.where(s >= 0, exp_v[b] * SLOTS + s, -1)
        gts[0, b] = gate_v[b].astype(jnp.float32)

    pl.semaphore_wait(barrier, 2)

    def remote(src, dst, ssem, rsem, dev):
        return pltpu.make_async_remote_copy(src_ref=src, dst_ref=dst, send_sem=ssem, recv_sem=rsem, device_id=dev, device_id_type=MESH)

    def exchange(buf, ssem, rsem):
        to_cross = remote(buf.at[0], buf.at[1], ssem.at[0], rsem.at[0], cross)
        to_sib = remote(buf.at[0], buf.at[2], ssem.at[1], rsem.at[1], sib)
        relay = remote(buf.at[1], buf.at[3], ssem.at[2], rsem.at[2], sib)
        return to_cross, to_sib, relay

    c_copies = exchange(codes, c_send.at[0], c_recv.at[0])
    g_copies = exchange(gts, c_send.at[1], c_recv.at[1])
    for cp in (*c_copies[:2], *g_copies[:2]):
        cp.start()

    x_f = x_v[...].astype(jnp.float32)
    normed = rms_norm(x_f, again[...].astype(jnp.float32).reshape(1, DIM))
    for i in range(NQ):
        q_cp[i].wait()
        qkv[i] = dot(normed, buf1[pl.ds(i * QCH, QCH), :], NT).astype(jnp.bfloat16)

    d_cp = []
    for n in range(NBLK):
        cp = pltpu.make_async_copy(wd.at[:, pl.ds(n * NB, NB)], buf1.at[:, pl.ds(n * NB, NB)], d_sem.at[n])
        cp.start(priority=1)
        d_cp.append(cp)

    c_copies[0].wait_recv()
    c_copies[2].start()
    g_copies[0].wait_recv()
    g_copies[2].start()

    q_row = lax.rem(lax.broadcasted_iota(jnp.int32, (4 * ROWS, ROWS), 0), ROWS)
    k_col = lax.broadcasted_iota(jnp.int32, (4 * ROWS, ROWS), 1)
    seen = (k_col <= q_row) & (k_col // SEQ == q_row // SEQ)
    lane_head = lax.broadcasted_iota(jnp.int32, (ROWS, 4 * HEAD), 1) // HEAD
    per = QCH // 256
    for g in range(DIM // 256):
        part = pl.ds((g % per) * 256, 256)
        q4 = qkv[g // per, :, part]
        k4 = qkv[NQ // 3 + g // per, :, part]
        v4 = qkv[2 * NQ // 3 + g // per, :, part]
        zero = jnp.zeros_like(q4)
        q_blocks = jnp.concatenate([jnp.where(lane_head == h, q4, zero) for h in range(4)], axis=0)
        s = dot(q_blocks, k4, NT) * (HEAD ** -0.5)
        s = jnp.where(seen, s, MASK_VALUE)
        ex = jnp.exp(s - jnp.max(s, axis=-1, keepdims=True))
        prob = (ex / jnp.sum(ex, axis=-1, keepdims=True)).astype(jnp.bfloat16)
        mixed = dot(prob, v4)
        c4 = mixed[0:ROWS]
        for h in range(1, 4):
            c4 = jnp.where(lane_head == h, mixed[h * ROWS:(h + 1) * ROWS], c4)
        ctx[:, pl.ds(g * 256, 256)] = c4.astype(jnp.bfloat16)

    for cp in o_cp:
        cp.wait()
    h = (x_f + dot(ctx[...], wo_v[...])).astype(jnp.bfloat16)
    resid[...] = h
    u_all[0] = rms_norm(h.astype(jnp.float32), mgain[...].astype(jnp.float32).reshape(1, DIM))

    u_copies = exchange(u_all, u_send, u_recv)
    u_copies[0].start()
    u_copies[1].start()

    for cp in (c_copies[1], c_copies[2], g_copies[1], g_copies[2]):
        cp.wait_recv()
    code = jnp.concatenate([codes[r, b] for r in range(GROUP) for b in range(2)], axis=1)
    gate = jnp.concatenate([gts[r, b] for r in range(GROUP) for b in range(2)], axis=1)
    block = lax.broadcasted_iota(jnp.int32, (TOP_K, TOKENS), 1) // SEQ
    code = jnp.where(code >= 0, code + block * (EXPERTS * SLOTS), -1)
    row = lax.broadcasted_iota(jnp.int32, (EROWS, TOKENS), 0)
    row_code = (row // SLOTS) * (EXPERTS * SLOTS) + lax.rem(row, SLOTS) + me * (LOCAL * SLOTS)

    def build(e, carry):
        want = row_code + e * SLOTS
        val = jnp.zeros((EROWS, TOKENS), jnp.float32)
        hit = jnp.zeros((EROWS, TOKENS), jnp.float32)
        for j in range(TOP_K):
            same = jnp.broadcast_to(code[j:j + 1, :], (EROWS, TOKENS)) == want
            val = jnp.where(same, jnp.broadcast_to(gate[j:j + 1, :], (EROWS, TOKENS)), val)
            hit = jnp.where(same, 1.0, hit)
        rows = pl.ds(pl.multiple_of(e * EROWS, EROWS), EROWS)
        disp[rows, :] = hit.astype(jnp.bfloat16)
        comb[rows, :] = val.astype(jnp.bfloat16)
        return carry

    lax.fori_loop(0, LOCAL, build, 0)
    comb_t = comb[...].T

    u_copies[0].wait_recv()
    u_copies[2].start()
    u_copies[1].wait_recv()
    u_copies[2].wait_recv()

    everyone = u_all[...].reshape(TOKENS, DIM)
    for n in range(DIM // 512):
        xg[:, pl.ds(n * 512, 512)] = dot(disp[...], everyone[:, n * 512:(n + 1) * 512]).astype(jnp.bfloat16)

    def expert(e, carry):
        pltpu.make_async_copy(wg.at[e], wg_v.at[e], g_sem.at[0, e]).wait()
        pltpu.make_async_copy(wu.at[e], wu_v.at[e], g_sem.at[1, e]).wait()
        rows = pl.ds(pl.multiple_of(e * EROWS, EROWS), EROWS)
        xe = xg[rows, :]
        gate_act = dot(xe, wg_v[e])
        up_act = dot(xe, wu_v[e])
        hid[rows, :] = (jax.nn.silu(gate_act) * up_act).astype(jnp.bfloat16)
        return carry

    lax.fori_loop(0, LOCAL, expert, 0)

    sends = []
    second = []

    def forward(n):
        first = sends[n]
        first.wait_recv()
        s_send[n] = s_send[n] + p_recv[n, pl.ds(ROWS, ROWS), :]
        cp = remote(s_send.at[n], r_recv.at[n], ss_sem.at[n], rr_sem.at[n], cross)
        cp.start()
        second.append(cp)

    for n in range(NBLK):
        cols = pl.ds(n * NB, NB)
        d_cp[n].wait()
        for e in range(LOCAL):
            o_v[pl.ds(e * EROWS, EROWS), :] = dot(hid[pl.ds(e * EROWS, EROWS), :], buf1[pl.ds(e * FFN, FFN), cols]).astype(jnp.bfloat16)
        part = dot(comb_t, o_v[...])
        keep[:, cols] = resid[:, cols].astype(jnp.float32) + part[0:ROWS]
        s_send[n] = part[ROWS:2 * ROWS]
        p_send[n] = part[2 * ROWS:]
        cp = remote(p_send.at[n], p_recv.at[n], ps_sem.at[n], pr_sem.at[n], sib)
        cp.start()
        sends.append(cp)
        if n >= 1:
            forward(n - 1)
    forward(NBLK - 1)

    for n in range(NBLK):
        cols = pl.ds(n * NB, NB)
        second[n].wait_recv()
        out_v[:, cols] = (keep[:, cols] + p_recv[n, pl.ds(0, ROWS), :] + r_recv[n]).astype(jnp.bfloat16)

    outs = [
        pltpu.make_async_copy(out_v.at[pl.ds(0, SEQ)], out_a, out_sem.at[0]),
        pltpu.make_async_copy(out_v.at[pl.ds(SEQ, SEQ)], out_b, out_sem.at[1]),
    ]
    for cp in outs:
        cp.start()
    for cp in (*c_copies, *g_copies, *u_copies, *sends, *second):
        cp.wait_send()
    for cp in outs:
        cp.wait()


def device_fn(tokens_a, experts_a, slots_a, gates_a, tokens_b, experts_b, slots_b, gates_b, attn_gain, w_query, w_key, w_value, w_out, moe_gain, w_gate, w_up, w_down):
    def by_row(w):
        return jnp.transpose(w, (1, 2, 0)).reshape(DIM, DIM)

    operands = (
        tokens_a, experts_a.T, slots_a.T, gates_a.T, tokens_b, experts_b.T, slots_b.T, gates_b.T, attn_gain, moe_gain,
        by_row(w_query), by_row(w_key), by_row(w_value), w_out.reshape(DIM, DIM), w_gate, w_up, w_down.reshape(LOCAL * FFN, DIM),
    )
    bf16, f32, i32 = jnp.bfloat16, jnp.float32, jnp.int32
    dma = pltpu.SemaphoreType.DMA
    scratch = [
        pltpu.VMEM((ROWS, DIM), bf16), pltpu.VMEM((2, TOP_K, SEQ), i32), pltpu.VMEM((2, TOP_K, SEQ), i32), pltpu.VMEM((2, TOP_K, SEQ), bf16),
        pltpu.VMEM((DIM,), bf16), pltpu.VMEM((DIM,), bf16),
        pltpu.VMEM((LOCAL * FFN, DIM), bf16), pltpu.VMEM((DIM, DIM), bf16), pltpu.VMEM((LOCAL, DIM, FFN), bf16), pltpu.VMEM((LOCAL, DIM, FFN), bf16),
        pltpu.VMEM((NQ, ROWS, QCH), bf16), pltpu.VMEM((ROWS, DIM), bf16), pltpu.VMEM((ROWS, DIM), bf16), pltpu.VMEM((GROUP, ROWS, DIM), bf16),
        pltpu.VMEM((GROUP, 2, TOP_K, SEQ), i32), pltpu.VMEM((GROUP, 2, TOP_K, SEQ), f32),
        pltpu.VMEM((XROWS, TOKENS), bf16), pltpu.VMEM((XROWS, TOKENS), bf16), pltpu.VMEM((XROWS, DIM), bf16), pltpu.VMEM((XROWS, FFN), bf16),
        pltpu.VMEM((XROWS, NB), bf16),
        pltpu.VMEM((NBLK, 2 * ROWS, NB), f32), pltpu.VMEM((NBLK, 2 * ROWS, NB), f32), pltpu.VMEM((NBLK, ROWS, NB), f32), pltpu.VMEM((NBLK, ROWS, NB), f32),
        pltpu.VMEM((ROWS, DIM), f32), pltpu.VMEM((ROWS, DIM), bf16),
        dma((10,)), dma((NQ,)), dma((NO,)), dma((2, LOCAL)), dma((NBLK,)), dma((2,)),
        dma((2, 3)), dma((2, 3)), dma((3,)), dma((3,)), dma((NBLK,)), dma((NBLK,)), dma((NBLK,)), dma((NBLK,)),
    ]
    shape = jax.ShapeDtypeStruct((SEQ, DIM), bf16)
    return pl.pallas_call(
        layer_kernel,
        out_shape=(shape, shape),
        in_specs=[pl.BlockSpec(memory_space=pl.ANY)] * len(operands),
        out_specs=[pl.BlockSpec(memory_space=pl.ANY)] * 2,
        scratch_shapes=scratch,
        compiler_params=pltpu.CompilerParams(collective_id=0, has_side_effects=True, vmem_limit_bytes=66_000_000),
        name="moe_layer",
    )(*operands)


def solution(mesh):
    row_spec = P(("dp", "ep"), None)
    full_spec = P(None, None, None)
    gain_spec = P(None)
    expert_spec = P("ep", None, None)
    in_specs = (row_spec, row_spec, row_spec, row_spec, row_spec, row_spec, row_spec, row_spec, gain_spec, full_spec, full_spec, full_spec, full_spec, gain_spec, expert_spec, expert_spec, expert_spec)
    return jax.shard_map(device_fn, mesh=mesh, in_specs=in_specs, out_specs=(row_spec, row_spec), check_vma=False)
```

time: 133 us -> 50.4 us (0.38)
  matrix products: 77.5 us -> 0 us
  Pallas kernels: 0 us -> 46.5 us
  waiting for transfers between devices: 19.3 us -> 0 us
  starting transfers between devices: 15.3 us -> 0 us
  local copies, waits for them, and re-layouts: 12.8 us -> 3.08 us
  other arithmetic: 6.49 us -> 0 us
    dot_general x14 -> x0, matrix products: 77.5 us -> none  [the longest x2 30.3 us: expert_ffn(): jnp.einsum('pecf,efd->pecd', hidden, w_down, preferred_element_type=jnp.f...]
    pallas_call x0 -> x1, Pallas kernels: none -> 46.5 us  [device_fn(): pl.pallas_call(layer_kernel, out_shape=(shape, shape), in_specs=[pl.Block...]
    all_to_all x4 -> x0, waiting for transfers between devices: 19.3 us -> none  [the longest x2 10.9 us: moe_layer(): returned = lax.all_to_all(expert_out, 'ep', 0, 0, tiled=True)]
    all_to_all x4 -> x0, starting transfers between devices: 15.3 us -> none  [the longest x2 8.01 us: moe_layer(): lax.all_to_all(dispatched, 'ep', 0, 0, tiled=True)]
    gather x4 -> x0, local copies, waits for them, and re-layouts: 6.99 us -> none  [the longest x2 4.45 us: dispatch_rows(): jnp.take(normed, source, axis=0, mode='fill', fill_value=0)]
    unnamed x26 -> x2, local copies, waits for them, and re-layouts: 0.26 us -> 3.08 us
    scatter x2 -> x0, local copies, waits for them, and re-layouts: 2.79 us -> none  [dispatch_rows(): jnp.full((experts_total * capacity,), seq_len, jnp.int32).at[dest_row]]
    convert_element_type x5 -> x0, other arithmetic: 2.28 us -> none  [the longest x2 1.33 us: combine_rows(): return (residual.astype(jnp.float32) + mixed_sum).astype(jnp.bfloat16)]
  transfers between devices with their start and end apart: 4 -> 0, of which waited for: 2 -> 0; matrix products, arithmetic and copies ran while one was open for 44% -> 0% of each run, Pallas kernels for 0% -> 0%
where the time goes in v1:
time: 50.4 us; the launch traced here: 50.2 us
  Pallas kernels  46.5 us (92%)
  local copies, waits for them, and re-layouts  3.08 us (6%)
  between operations  0.65 us (1%)
    pallas_call x1, Pallas kernels, device_fn(): pl.pallas_call(layer_kernel, out_shape=(shape, shape), in_specs=[pl.Block...  46.5 us
    unnamed x2, local copies, waits for them, and re-layouts  3.08 us

profile of v1, /device:TPU:0, one launch (start us, length us, event | category | flops | bytes accessed | tf_op | source)
XLA Modules:
  0.0 50.2 jit_solution(1694306923030097785)
XLA Ops:
  0.6 46.5 %moe_layer.1 = (bf16[32,1536]{1,0:T(8,128)(2,1)}, bf16[32,1536]{1,0:T(8,128)(2,1)}) custom-call(bf16[32,1536]{1,0:T(8,128)(2,1)} %tok_a.1, s32[8,32]{1,0:T(8,128)} %bitcast.22, s32[8,32]{1,0:T(8,128)} %bitcast.23, bf16[8,32]{1,0:T(8,128)(2,1)} %bitcast.26, bf16[32,1536]{1,0:T(8,128)(2,1)} %tok_b.1, s32[8,32]{1,0:T(8,128)} %bitcast.24, s32[8,32]{1,0:T(8,128)} %bitcast.25, ...), custom_call_target="tpu_custom_call" | custom-call | tf_op jit(solution)/shard_map/moe_layer/pallas_call | solution.py:276
  47.1 1.5 %copy.21 = bf16[32,1536]{1,0:T(8,128)(2,1)} copy(bf16[32,1536]{1,0:T(8,128)(2,1)} %get-tuple-element.4) | data formatting | bytes 196608
  48.7 1.5 %copy.22 = bf16[32,1536]{1,0:T(8,128)(2,1)} copy(bf16[32,1536]{1,0:T(8,128)(2,1)} %get-tuple-element.5) | data formatting | bytes 196608

commit v2 on v1

v2 whole, which is shorter than its diff:
```python
import functools

import jax
import jax.numpy as jnp
from jax import lax
from jax.experimental import pallas as pl
from jax.experimental.pallas import tpu as pltpu
from jax.sharding import PartitionSpec as P

NORM_EPS = 1e-6
MASK_VALUE = -1e30
MESH = pl.DeviceIdType.MESH
VMEM_LIMIT = 65_000_000

SEQ = 32
ROWS = 2 * SEQ
TOP_K = 8
DIM = 1536
HEAD = 64
FFN = 512
SLOTS = 8
LOCAL = 10
EXPERTS = 40
GROUP = 4
TOKENS = GROUP * ROWS
EROWS = GROUP * 2 * SLOTS
RROWS = LOCAL * 2 * SLOTS
NB = 256
NBLK = DIM // NB
QCH = 768
PER = DIM // QCH
NQ = 3 * PER

NT = (((1,), (1,)), ((), ()))
NN = (((1,), (0,)), ((), ()))


def dot(lhs, rhs, dims=NN):
    return lax.dot_general(lhs, rhs, dims, preferred_element_type=jnp.float32)


def rms_norm(rows_f, gain):
    inv_rms = lax.rsqrt(jnp.mean(rows_f * rows_f, axis=-1, keepdims=True) + NORM_EPS)
    return (rows_f * inv_rms * gain).astype(jnp.bfloat16)


def layer_kernel(
    tok_a, exp_a, slot_a, gate_a, tok_b, exp_b, slot_b, gate_b, again_h, mgain_h, wq, wk, wv, wo, wg, wu, wd,
    out_h,
    x_v, exp_v, slot_v, gate_v, again, mgain, buf1, wo_v, wg_v, wu_v, qkv, ctx, u_all, codes, gts, disp, comb_t, xg, hid, o_v,
    p_send, p_recv, s_send, r_recv, keep, out_v,
    in_sem, q_sem, o_sem, g_sem, d_sem, out_sem, c_send, c_recv, u_send, u_recv, ps_sem, pr_sem, ss_sem, rr_sem,
):
    me = lax.axis_index("ep")
    dp = lax.axis_index("dp")
    x_pos = me // 2
    core = lax.rem(me, 2)
    sib = (dp, x_pos * 2 + (1 - core))
    cross = (dp, (1 - x_pos) * 2 + core)

    ins = []
    for i, (src, dst) in enumerate([
        (tok_a, x_v.at[pl.ds(0, SEQ)]), (tok_b, x_v.at[pl.ds(SEQ, SEQ)]), (again_h, again),
        (exp_a, exp_v.at[0]), (exp_b, exp_v.at[1]), (slot_a, slot_v.at[0]), (slot_b, slot_v.at[1]),
        (gate_a, gate_v.at[0]), (gate_b, gate_v.at[1]), (mgain_h, mgain),
    ]):
        cp = pltpu.make_async_copy(src, dst, in_sem.at[i])
        cp.start()
        ins.append(cp)

    q_cp = []
    for i in range(NQ):
        w, r = (wq, wk, wv)[i // PER], i % PER
        cp = pltpu.make_async_copy(w.at[pl.ds(r * QCH, QCH)], buf1.at[pl.ds(i * QCH, QCH)], q_sem.at[i])
        cp.start(priority=1)
        q_cp.append(cp)
    o_cp = pltpu.make_async_copy(wo, wo_v, o_sem.at[0])
    o_cp.start(priority=1)

    g_cp = [
        (pltpu.make_async_copy(wg.at[e], wg_v.at[e], g_sem.at[0, e]), pltpu.make_async_copy(wu.at[e], wu_v.at[e], g_sem.at[1, e]))
        for e in range(LOCAL)
    ]

    def fetch(first, last):
        for e in range(first, last):
            for cp in g_cp[e]:
                cp.start(priority=1)

    barrier = pltpu.get_barrier_semaphore()
    for peer in (sib, cross):
        pl.semaphore_signal(barrier, inc=1, device_id=peer, device_id_type=MESH)

    for cp in ins:
        cp.wait()

    for b in range(2):
        s = slot_v[b]
        codes[0, b] = jnp.where(s >= 0, exp_v[b] * SLOTS + s, -1)
        gts[0, b] = gate_v[b].astype(jnp.float32)

    def remote(src, dst, ssem, rsem, dev):
        return pltpu.make_async_remote_copy(src_ref=src, dst_ref=dst, send_sem=ssem, recv_sem=rsem, device_id=dev, device_id_type=MESH)

    def exchange(buf, ssem, rsem):
        to_cross = remote(buf.at[0], buf.at[1], ssem.at[0], rsem.at[0], cross)
        to_sib = remote(buf.at[0], buf.at[2], ssem.at[1], rsem.at[1], sib)
        relay = remote(buf.at[1], buf.at[3], ssem.at[2], rsem.at[2], sib)
        return to_cross, to_sib, relay

    x_f = x_v[...].astype(jnp.float32)
    normed = rms_norm(x_f, again[...].astype(jnp.float32).reshape(1, DIM))

    def project(first, last):
        rows = pl.ds(first * QCH, (last - first) * QCH)
        res = dot(normed, buf1[rows, :], NT).astype(jnp.bfloat16)
        for i in range(first, last):
            qkv[i] = res[:, (i - first) * QCH:(i - first + 1) * QCH]

    q_cp[0].wait()
    fetch(0, 1)
    project(0, 1)
    q_cp[1].wait()
    fetch(1, 2)
    project(1, 2)

    q_cp[2].wait()
    q_cp[3].wait()
    fetch(2, 4)
    project(2, 4)

    pl.semaphore_wait(barrier, 2)
    c_copies = exchange(codes, c_send.at[0], c_recv.at[0])
    g_copies = exchange(gts, c_send.at[1], c_recv.at[1])
    for cp in (*c_copies[:2], *g_copies[:2]):
        cp.start()

    q_cp[4].wait()
    q_cp[5].wait()
    fetch(4, LOCAL)
    q_row = lax.rem(lax.broadcasted_iota(jnp.int32, (4 * ROWS, ROWS), 0), ROWS)
    k_col = lax.broadcasted_iota(jnp.int32, (4 * ROWS, ROWS), 1)
    seen = (k_col <= q_row) & (k_col // SEQ == q_row // SEQ)
    lane_head = lax.broadcasted_iota(jnp.int32, (ROWS, 4 * HEAD), 1) // HEAD
    groups = QCH // 256
    probs = []
    for g in range(DIM // 256):
        part = pl.ds((g % groups) * 256, 256)
        q4 = qkv[g // groups, :, part]
        k4 = qkv[PER + g // groups, :, part]
        zero = jnp.zeros_like(q4)
        q_blocks = jnp.concatenate([jnp.where(lane_head == h, q4, zero) for h in range(4)], axis=0)
        s = dot(q_blocks, k4, NT) * (HEAD ** -0.5)
        s = jnp.where(seen, s, MASK_VALUE)
        ex = jnp.exp(s - jnp.max(s, axis=-1, keepdims=True))
        probs.append((ex / jnp.sum(ex, axis=-1, keepdims=True)).astype(jnp.bfloat16))
    project(4, 6)
    for g in range(DIM // 256):
        v4 = qkv[2 * PER + g // groups, :, pl.ds((g % groups) * 256, 256)]
        mixed = dot(probs[g], v4)
        c4 = mixed[0:ROWS]
        for h in range(1, 4):
            c4 = jnp.where(lane_head == h, mixed[h * ROWS:(h + 1) * ROWS], c4)
        ctx[:, pl.ds(g * 256, 256)] = c4.astype(jnp.bfloat16)

    o_cp.wait()
    h = (x_f + dot(ctx[...], wo_v[...])).astype(jnp.bfloat16)
    keep[...] = h.astype(jnp.float32)
    u_all[0] = rms_norm(h.astype(jnp.float32), mgain[...].astype(jnp.float32).reshape(1, DIM))

    u_copies = exchange(u_all, u_send, u_recv)
    u_copies[0].start()
    u_copies[1].start()

    d_cp = []
    for n in range(NBLK):
        cp = pltpu.make_async_copy(wd.at[:, pl.ds(n * NB, NB)], buf1.at[:, pl.ds(n * NB, NB)], d_sem.at[n])
        cp.start(priority=1)
        d_cp.append(cp)

    c_copies[0].wait_recv()
    c_copies[2].start()
    g_copies[0].wait_recv()
    g_copies[2].start()
    for cp in (c_copies[1], g_copies[1], c_copies[2], g_copies[2]):
        cp.wait_recv()
    row = lax.broadcasted_iota(jnp.int32, (RROWS, ROWS), 0)
    want = (row // (2 * SLOTS) + me * LOCAL) * SLOTS + lax.rem(row, SLOTS) + lax.rem(row // SLOTS, 2) * (EXPERTS * SLOTS)
    for r in range(GROUP):
        code = jnp.concatenate([codes[r, 0], jnp.where(codes[r, 1] >= 0, codes[r, 1] + EXPERTS * SLOTS, -1)], axis=1)
        gate = jnp.concatenate([gts[r, 0], gts[r, 1]], axis=1)
        val = jnp.zeros((RROWS, ROWS), jnp.float32)
        hit = jnp.zeros((RROWS, ROWS), jnp.float32)
        for j in range(TOP_K):
            same = jnp.broadcast_to(code[j:j + 1, :], (RROWS, ROWS)) == want
            val = jnp.where(same, jnp.broadcast_to(gate[j:j + 1, :], (RROWS, ROWS)), val)
            hit = jnp.where(same, 1.0, hit)
        disp[r] = hit.astype(jnp.bfloat16)
        comb_t[r] = val.T.astype(jnp.bfloat16)

    def gather(r):
        xg[r] = dot(disp[r], u_all[r]).astype(jnp.bfloat16).reshape(LOCAL, 2 * SLOTS, DIM)

    gather(0)
    u_copies[1].wait_recv()
    gather(2)
    u_copies[0].wait_recv()
    u_copies[2].start()
    gather(1)
    u_copies[2].wait_recv()
    gather(3)

    def expert(e):
        xe = xg[:, e].reshape(EROWS, DIM)
        gate_act = dot(xe, wg_v[e])
        up_act = dot(xe, wu_v[e])
        hid[:, e] = (jax.nn.silu(gate_act) * up_act).astype(jnp.bfloat16).reshape(GROUP, 2 * SLOTS, FFN)

    for first, last in ((0, 7), (7, LOCAL)):
        for e in range(first, last):
            for cp in g_cp[e]:
                cp.wait()
        for e in range(first, last):
            expert(e)

    sends = []
    second = []

    def forward(n):
        sends[n].wait_recv()
        s_send[n] = s_send[n] + p_recv[n, 1]
        cp = remote(s_send.at[n], r_recv.at[n], ss_sem.at[n], rr_sem.at[n], cross)
        cp.start()
        second.append(cp)

    def down(n):
        cols = pl.ds(n * NB, NB)
        for e in range(LOCAL):
            res = dot(hid[:, e].reshape(EROWS, FFN), buf1[pl.ds(e * FFN, FFN), cols])
            o_v[n % 2, :, e] = res.astype(jnp.bfloat16).reshape(GROUP, 2 * SLOTS, NB)

    def combine(n, r):
        return dot(comb_t[r], o_v[n % 2, r].reshape(RROWS, NB))

    d_cp[0].wait()
    down(0)
    for n in range(NBLK):
        if n + 1 < NBLK:
            d_cp[n + 1].wait()
        p_send[n, 1] = combine(n, 3)
        p_send[n, 0] = combine(n, 2)
        s_send[n] = combine(n, 1)
        cols = pl.ds(n * NB, NB)
        keep[:, cols] = keep[:, cols] + combine(n, 0)
        if n + 1 < NBLK:
            down(n + 1)
        cp = remote(p_send.at[n], p_recv.at[n], ps_sem.at[n], pr_sem.at[n], sib)
        cp.start()
        sends.append(cp)
        if n >= 1:
            forward(n - 1)
    forward(NBLK - 1)

    for n in range(NBLK):
        cols = pl.ds(n * NB, NB)
        second[n].wait_recv()
        out_v[:, cols] = (keep[:, cols] + p_recv[n, 0] + r_recv[n]).astype(jnp.bfloat16)

    out_cp = pltpu.make_async_copy(out_v, out_h, out_sem.at[0])
    out_cp.start()
    for cp in (*c_copies, *g_copies, *u_copies, *sends, *second):
        cp.wait_send()
    out_cp.wait()


def device_fn(tokens_a, experts_a, slots_a, gates_a, tokens_b, experts_b, slots_b, gates_b, attn_gain, w_query, w_key, w_value, w_out, moe_gain, w_gate, w_up, w_down):
    def by_row(w):
        return jnp.transpose(w, (1, 2, 0)).reshape(DIM, DIM)

    operands = (
        tokens_a, experts_a.T, slots_a.T, gates_a.T, tokens_b, experts_b.T, slots_b.T, gates_b.T, attn_gain, moe_gain,
        by_row(w_query), by_row(w_key), by_row(w_value), w_out.reshape(DIM, DIM), w_gate, w_up, w_down.reshape(LOCAL * FFN, DIM),
    )
    bf16, f32, i32 = jnp.bfloat16, jnp.float32, jnp.int32
    dma = pltpu.SemaphoreType.DMA
    scratch = [
        pltpu.VMEM((ROWS, DIM), bf16), pltpu.VMEM((2, TOP_K, SEQ), i32), pltpu.VMEM((2, TOP_K, SEQ), i32), pltpu.VMEM((2, TOP_K, SEQ), bf16),
        pltpu.VMEM((DIM,), bf16), pltpu.VMEM((DIM,), bf16),
        pltpu.VMEM((LOCAL * FFN, DIM), bf16), pltpu.VMEM((DIM, DIM), bf16), pltpu.VMEM((LOCAL, DIM, FFN), bf16), pltpu.VMEM((LOCAL, DIM, FFN), bf16),
        pltpu.VMEM((NQ, ROWS, QCH), bf16), pltpu.VMEM((ROWS, DIM), bf16), pltpu.VMEM((GROUP, ROWS, DIM), bf16),
        pltpu.VMEM((GROUP, 2, TOP_K, SEQ), i32), pltpu.VMEM((GROUP, 2, TOP_K, SEQ), f32),
        pltpu.VMEM((GROUP, RROWS, ROWS), bf16), pltpu.VMEM((GROUP, ROWS, RROWS), bf16),
        pltpu.VMEM((GROUP, LOCAL, 2 * SLOTS, DIM), bf16), pltpu.VMEM((GROUP, LOCAL, 2 * SLOTS, FFN), bf16), pltpu.VMEM((2, GROUP, LOCAL, 2 * SLOTS, NB), bf16),
        pltpu.VMEM((NBLK, 2, ROWS, NB), f32), pltpu.VMEM((NBLK, 2, ROWS, NB), f32), pltpu.VMEM((NBLK, ROWS, NB), f32), pltpu.VMEM((NBLK, ROWS, NB), f32),
        pltpu.VMEM((ROWS, DIM), f32), pltpu.VMEM((ROWS, DIM), bf16),
        dma((10,)), dma((NQ,)), dma((1,)), dma((2, LOCAL)), dma((NBLK,)), dma((1,)),
        dma((2, 3)), dma((2, 3)), dma((3,)), dma((3,)), dma((NBLK,)), dma((NBLK,)), dma((NBLK,)), dma((NBLK,)),
    ]
    both = pl.pallas_call(
        layer_kernel,
        out_shape=jax.ShapeDtypeStruct((ROWS, DIM), bf16),
        in_specs=[pl.BlockSpec(memory_space=pl.ANY)] * len(operands),
        out_specs=pl.BlockSpec(memory_space=pl.ANY),
        scratch_shapes=scratch,
        compiler_params=pltpu.CompilerParams(collective_id=0, has_side_effects=True, vmem_limit_bytes=VMEM_LIMIT),
        name="moe_layer",
    )(*operands)
    return split(both)


def split_kernel(both, out_a, out_b, sem):
    copies = [pltpu.make_async_copy(both.at[pl.ds(i * SEQ, SEQ)], dst, sem.at[i]) for i, dst in enumerate((out_a, out_b))]
    for cp in copies:
        cp.start()
    for cp in copies:
        cp.wait()


def split(both):
    shape = jax.ShapeDtypeStruct((SEQ, DIM), jnp.bfloat16)
    return pl.pallas_call(
        split_kernel,
        out_shape=(shape, shape),
        in_specs=[pl.BlockSpec(memory_space=pltpu.VMEM)],
        out_specs=[pl.BlockSpec(memory_space=pl.ANY)] * 2,
        scratch_shapes=[pltpu.SemaphoreType.DMA((2,))],
        name="split",
    )(both)


def solution(mesh):
    row_spec = P(("dp", "ep"), None)
    full_spec = P(None, None, None)
    gain_spec = P(None)
    expert_spec = P("ep", None, None)
    in_specs = (row_spec, row_spec, row_spec, row_spec, row_spec, row_spec, row_spec, row_spec, gain_spec, full_spec, full_spec, full_spec, full_spec, gain_spec, expert_spec, expert_spec, expert_spec)
    return jax.shard_map(device_fn, mesh=mesh, in_specs=in_specs, out_specs=(row_spec, row_spec), check_vma=False)
```

time: 50.4 us -> 38.7 us (0.77)
  Pallas kernels: 46.5 us -> 37.9 us
  local copies, waits for them, and re-layouts: 3.08 us -> 0 us
    pallas_call x1 -> x2, Pallas kernels: 46.5 us -> 37.9 us  [the longest x1 36.3 us: device_fn(): pl.pallas_call(layer_kernel, out_shape=jax.ShapeDtypeStruct((ROWS, DIM),...]
    unnamed x2 -> x0, local copies, waits for them, and re-layouts: 3.08 us -> none
where the time goes in v2:
time: 38.7 us; the launch traced here: 38.6 us
  Pallas kernels  37.9 us (98%)
  between operations  0.65 us (2%)
    pallas_call x1, Pallas kernels, device_fn(): pl.pallas_call(layer_kernel, out_shape=jax.ShapeDtypeStruct((ROWS, DIM),...  36.3 us
    pallas_call x1, Pallas kernels, split(): pl.pallas_call(split_kernel, out_shape=(shape, shape), in_specs=[pl.Block...  1.62 us

profile of v2, /device:TPU:0, one launch (start us, length us, event | category | flops | bytes accessed | tf_op | source)
XLA Modules:
  0.0 38.6 jit_solution(10438377814527333622)
XLA Ops:
  0.6 36.3 %moe_layer.1.both = bf16[64,1536]{1,0:T(8,128)(2,1)} custom-call(bf16[32,1536]{1,0:T(8,128)(2,1)} %tok_a.1, s32[8,32]{1,0:T(8,128)} %bitcast.22, s32[8,32]{1,0:T(8,128)} %bitcast.23, bf16[8,32]{1,0:T(8,128)(2,1)} %bitcast.26, bf16[32,1536]{1,0:T(8,128)(2,1)} %tok_b.1, s32[8,32]{1,0:T(8,128)} %bitcast.24, s32[8,32]{1,0:T(8,128)} %bitcast.25, ...), custom_call_target="tpu_custom_call" | custom-call | tf_op jit(solution)/shard_map/moe_layer/pallas_call | solution.py:299
  37.0 1.6 %split.1 = (bf16[32,1536]{1,0:T(8,128)(2,1)}, bf16[32,1536]{1,0:T(8,128)(2,1)}) custom-call(bf16[64,1536]{1,0:T(8,128)(2,1)} %moe_layer.1.both), custom_call_target="tpu_custom_call" | custom-call | tf_op jit(solution)/shard_map/split/pallas_call | solution.py:321

commit v3 on v2

--- a/solution.py
+++ b/solution.py
@@ -10,7 +10,7 @@
 NORM_EPS = 1e-6
 MASK_VALUE = -1e30
 MESH = pl.DeviceIdType.MESH
-VMEM_LIMIT = 65_000_000
+VMEM_LIMIT = 66_000_000
 
 SEQ = 32
 ROWS = 2 * SEQ
@@ -25,6 +25,8 @@
 TOKENS = GROUP * ROWS
 EROWS = GROUP * 2 * SLOTS
 RROWS = LOCAL * 2 * SLOTS
+KS = (256, 256, 512, 512)
+KOFF = tuple(sum(KS[:k]) for k in range(len(KS)))
 NB = 256
 NBLK = DIM // NB
 QCH = 768
@@ -48,7 +50,7 @@
     tok_a, exp_a, slot_a, gate_a, tok_b, exp_b, slot_b, gate_b, again_h, mgain_h, wq, wk, wv, wo, wg, wu, wd,
     out_h,
     x_v, exp_v, slot_v, gate_v, again, mgain, buf1, wo_v, wg_v, wu_v, qkv, ctx, u_all, codes, gts, disp, comb_t, xg, hid, o_v,
-    p_send, p_recv, s_send, r_recv, keep, out_v,
+    p_send, p_recv, s_send, r_recv, keep, out_v, acc,
     in_sem, q_sem, o_sem, g_sem, d_sem, out_sem, c_send, c_recv, u_send, u_recv, ps_sem, pr_sem, ss_sem, rr_sem,
 ):
     me = lax.axis_index("ep")
@@ -77,15 +79,14 @@
     o_cp = pltpu.make_async_copy(wo, wo_v, o_sem.at[0])
     o_cp.start(priority=1)
 
-    g_cp = [
-        (pltpu.make_async_copy(wg.at[e], wg_v.at[e], g_sem.at[0, e]), pltpu.make_async_copy(wu.at[e], wu_v.at[e], g_sem.at[1, e]))
-        for e in range(LOCAL)
-    ]
-
-    def fetch(first, last):
-        for e in range(first, last):
-            for cp in g_cp[e]:
-                cp.start(priority=1)
+    g_cp = []
+    for k, (off, size) in enumerate(zip(KOFF, KS)):
+        ks = pl.ds(off, size)
+        g_cp.append([pltpu.make_async_copy(w.at[:, ks, :], v.at[:, ks, :], g_sem.at[i, k]) for i, (w, v) in enumerate(((wg, wg_v), (wu, wu_v)))])
+
+    def fetch(k):
+        for cp in g_cp[k]:
+            cp.start(priority=1)
 
     barrier = pltpu.get_barrier_semaphore()
     for peer in (sib, cross):
@@ -118,15 +119,15 @@
             qkv[i] = res[:, (i - first) * QCH:(i - first + 1) * QCH]
 
     q_cp[0].wait()
-    fetch(0, 1)
+    fetch(0)
     project(0, 1)
     q_cp[1].wait()
-    fetch(1, 2)
+    fetch(1)
     project(1, 2)
 
     q_cp[2].wait()
     q_cp[3].wait()
-    fetch(2, 4)
+    fetch(2)
     project(2, 4)
 
     pl.semaphore_wait(barrier, 2)
@@ -137,7 +138,7 @@
 
     q_cp[4].wait()
     q_cp[5].wait()
-    fetch(4, LOCAL)
+    fetch(3)
     q_row = lax.rem(lax.broadcasted_iota(jnp.int32, (4 * ROWS, ROWS), 0), ROWS)
     k_col = lax.broadcasted_iota(jnp.int32, (4 * ROWS, ROWS), 1)
     seen = (k_col <= q_row) & (k_col // SEQ == q_row // SEQ)
@@ -168,9 +169,13 @@
     keep[...] = h.astype(jnp.float32)
     u_all[0] = rms_norm(h.astype(jnp.float32), mgain[...].astype(jnp.float32).reshape(1, DIM))
 
-    u_copies = exchange(u_all, u_send, u_recv)
-    u_copies[0].start()
-    u_copies[1].start()
+    u_copies = []
+    for k, (off, size) in enumerate(zip(KOFF, KS)):
+        view = u_all.at[:, :, pl.ds(off, size)]
+        u_copies.append(exchange(view, u_send.at[k], u_recv.at[k]))
+        u_copies[k][0].start()
+    for copies in u_copies:
+        copies[1].start()
 
     d_cp = []
     for n in range(NBLK):
@@ -198,36 +203,54 @@
         disp[r] = hit.astype(jnp.bfloat16)
         comb_t[r] = val.T.astype(jnp.bfloat16)
 
-    def gather(r):
-        xg[r] = dot(disp[r], u_all[r]).astype(jnp.bfloat16).reshape(LOCAL, 2 * SLOTS, DIM)
-
-    gather(0)
-    u_copies[1].wait_recv()
-    gather(2)
-    u_copies[0].wait_recv()
-    u_copies[2].start()
-    gather(1)
-    u_copies[2].wait_recv()
-    gather(3)
-
-    def expert(e):
-        xe = xg[:, e].reshape(EROWS, DIM)
-        gate_act = dot(xe, wg_v[e])
-        up_act = dot(xe, wu_v[e])
-        hid[:, e] = (jax.nn.silu(gate_act) * up_act).astype(jnp.bfloat16).reshape(GROUP, 2 * SLOTS, FFN)
-
-    for first, last in ((0, 7), (7, LOCAL)):
+    def gather(r, k):
+        ks = pl.ds(KOFF[k], KS[k])
+        xg[r, :, :, ks] = dot(disp[r], u_all[r, :, ks]).astype(jnp.bfloat16).reshape(LOCAL, 2 * SLOTS, KS[k])
+
+    for k in range(len(KS)):
+        gather(0, k)
+    for k in range(len(KS)):
+        u_copies[k][1].wait_recv()
+    for k in range(len(KS)):
+        gather(2, k)
+
+    def relay(k):
+        u_copies[k][0].wait_recv()
+        u_copies[k][2].start()
+
+    def experts(k, first, last):
+        ks = pl.ds(KOFF[k], KS[k])
         for e in range(first, last):
-            for cp in g_cp[e]:
-                cp.wait()
-        for e in range(first, last):
-            expert(e)
+            xe = xg[:, e, :, ks].reshape(EROWS, KS[k])
+            gate_act = dot(xe, wg_v[e, ks, :])
+            up_act = dot(xe, wu_v[e, ks, :])
+            if k > 0:
+                gate_act = acc[e, 0] + gate_act
+                up_act = acc[e, 1] + up_act
+            if k + 1 < len(KS):
+                acc[e, 0] = gate_act
+                acc[e, 1] = up_act
+            else:
+                hid[:, e] = (jax.nn.silu(gate_act) * up_act).astype(jnp.bfloat16).reshape(GROUP, 2 * SLOTS, FFN)
+
+    relay(0)
+    for k in range(len(KS)):
+        gather(1, k)
+        u_copies[k][2].wait_recv()
+        for cp in g_cp[k]:
+            cp.wait()
+        gather(3, k)
+        half = LOCAL // 2
+        experts(k, 0, half)
+        if k + 1 < len(KS):
+            relay(k + 1)
+        experts(k, half, LOCAL)
 
     sends = []
     second = []
 
     def forward(n):
-        sends[n].wait_recv()
+        sends[n][0].wait_recv()
         s_send[n] = s_send[n] + p_recv[n, 1]
         cp = remote(s_send.at[n], r_recv.at[n], ss_sem.at[n], rr_sem.at[n], cross)
         cp.start()
@@ -254,21 +277,22 @@
         keep[:, cols] = keep[:, cols] + combine(n, 0)
         if n + 1 < NBLK:
             down(n + 1)
-        cp = remote(p_send.at[n], p_recv.at[n], ps_sem.at[n], pr_sem.at[n], sib)
-        cp.start()
-        sends.append(cp)
+        sends.append([remote(p_send.at[n, i], p_recv.at[n, i], ps_sem.at[n, i], pr_sem.at[n, i], sib) for i in (1, 0)])
+        for cp in sends[n]:
+            cp.start()
         if n >= 1:
             forward(n - 1)
     forward(NBLK - 1)
 
     for n in range(NBLK):
         cols = pl.ds(n * NB, NB)
+        sends[n][1].wait_recv()
         second[n].wait_recv()
         out_v[:, cols] = (keep[:, cols] + p_recv[n, 0] + r_recv[n]).astype(jnp.bfloat16)
 
     out_cp = pltpu.make_async_copy(out_v, out_h, out_sem.at[0])
     out_cp.start()
-    for cp in (*c_copies, *g_copies, *u_copies, *sends, *second):
+    for cp in (*c_copies, *g_copies, *(c for cs in u_copies for c in cs), *(c for cs in sends for c in cs), *second):
         cp.wait_send()
     out_cp.wait()
 
@@ -292,9 +316,9 @@
         pltpu.VMEM((GROUP, RROWS, ROWS), bf16), pltpu.VMEM((GROUP, ROWS, RROWS), bf16),
         pltpu.VMEM((GROUP, LOCAL, 2 * SLOTS, DIM), bf16), pltpu.VMEM((GROUP, LOCAL, 2 * SLOTS, FFN), bf16), pltpu.VMEM((2, GROUP, LOCAL, 2 * SLOTS, NB), bf16),
         pltpu.VMEM((NBLK, 2, ROWS, NB), f32), pltpu.VMEM((NBLK, 2, ROWS, NB), f32), pltpu.VMEM((NBLK, ROWS, NB), f32), pltpu.VMEM((NBLK, ROWS, NB), f32),
-        pltpu.VMEM((ROWS, DIM), f32), pltpu.VMEM((ROWS, DIM), bf16),
-        dma((10,)), dma((NQ,)), dma((1,)), dma((2, LOCAL)), dma((NBLK,)), dma((1,)),
-        dma((2, 3)), dma((2, 3)), dma((3,)), dma((3,)), dma((NBLK,)), dma((NBLK,)), dma((NBLK,)), dma((NBLK,)),
+        pltpu.VMEM((ROWS, DIM), f32), pltpu.VMEM((ROWS, DIM), bf16), pltpu.VMEM((LOCAL, 2, EROWS, FFN), f32),
+        dma((10,)), dma((NQ,)), dma((1,)), dma((2, len(KS))), dma((NBLK,)), dma((1,)),
+        dma((2, 3)), dma((2, 3)), dma((len(KS), 3)), dma((len(KS), 3)), dma((NBLK, 2)), dma((NBLK, 2)), dma((NBLK,)), dma((NBLK,)),
     ]
     both = pl.pallas_call(
         layer_kernel,

time: 38.7 us -> 37.5 us (0.969)
  Pallas kernels: 37.9 us -> 36.7 us
    pallas_call x1, Pallas kernels: 36.3 us -> 35.1 us  [device_fn(): pl.pallas_call(layer_kernel, out_shape=jax.ShapeDtypeStruct((ROWS, DIM),...]
where the time goes in v3:
time: 37.5 us; the launch traced here: 37.4 us
  Pallas kernels  36.7 us (98%)
  between operations  0.65 us (2%)
    pallas_call x1, Pallas kernels, device_fn(): pl.pallas_call(layer_kernel, out_shape=jax.ShapeDtypeStruct((ROWS, DIM),...  35.1 us
    pallas_call x1, Pallas kernels, split(): pl.pallas_call(split_kernel, out_shape=(shape, shape), in_specs=[pl.Block...  1.62 us

profile of v3, /device:TPU:0, one launch (start us, length us, event | category | flops | bytes accessed | tf_op | source)
XLA Modules:
  0.0 37.4 jit_solution(15873776258922071550)
XLA Ops:
  0.6 35.1 %moe_layer.1.both = bf16[64,1536]{1,0:T(8,128)(2,1)} custom-call(bf16[32,1536]{1,0:T(8,128)(2,1)} %tok_a.1, s32[8,32]{1,0:T(8,128)} %bitcast.22, s32[8,32]{1,0:T(8,128)} %bitcast.23, bf16[8,32]{1,0:T(8,128)(2,1)} %bitcast.26, bf16[32,1536]{1,0:T(8,128)(2,1)} %tok_b.1, s32[8,32]{1,0:T(8,128)} %bitcast.24, s32[8,32]{1,0:T(8,128)} %bitcast.25, ...), custom_call_target="tpu_custom_call" | custom-call | tf_op jit(solution)/shard_map/moe_layer/pallas_call | solution.py:323
  35.8 1.6 %split.1 = (bf16[32,1536]{1,0:T(8,128)(2,1)}, bf16[32,1536]{1,0:T(8,128)(2,1)}) custom-call(bf16[64,1536]{1,0:T(8,128)(2,1)} %moe_layer.1.both), custom_call_target="tpu_custom_call" | custom-call | tf_op jit(solution)/shard_map/split/pallas_call | solution.py:345

commit v4 on v3

--- a/solution.py
+++ b/solution.py
@@ -27,9 +27,10 @@
 RROWS = LOCAL * 2 * SLOTS
 KS = (256, 256, 512, 512)
 KOFF = tuple(sum(KS[:k]) for k in range(len(KS)))
-NB = 256
-NBLK = DIM // NB
-QCH = 768
+NBS = (128, 256, 256, 256, 256, 256, 128)
+NOFF = tuple(sum(NBS[:n]) for n in range(len(NBS)))
+NBLK = len(NBS)
+QCH = 512
 PER = DIM // QCH
 NQ = 3 * PER
 
@@ -122,13 +123,14 @@
     fetch(0)
     project(0, 1)
     q_cp[1].wait()
+    q_cp[2].wait()
     fetch(1)
-    project(1, 2)
-
-    q_cp[2].wait()
-    q_cp[3].wait()
+    project(1, 3)
+
+    for i in (3, 4, 5):
+        q_cp[i].wait()
     fetch(2)
-    project(2, 4)
+    project(3, 6)
 
     pl.semaphore_wait(barrier, 2)
     c_copies = exchange(codes, c_send.at[0], c_recv.at[0])
@@ -136,8 +138,8 @@
     for cp in (*c_copies[:2], *g_copies[:2]):
         cp.start()
 
-    q_cp[4].wait()
-    q_cp[5].wait()
+    for i in (6, 7, 8):
+        q_cp[i].wait()
     fetch(3)
     q_row = lax.rem(lax.broadcasted_iota(jnp.int32, (4 * ROWS, ROWS), 0), ROWS)
     k_col = lax.broadcasted_iota(jnp.int32, (4 * ROWS, ROWS), 1)
@@ -155,7 +157,8 @@
         s = jnp.where(seen, s, MASK_VALUE)
         ex = jnp.exp(s - jnp.max(s, axis=-1, keepdims=True))
         probs.append((ex / jnp.sum(ex, axis=-1, keepdims=True)).astype(jnp.bfloat16))
-    project(4, 6)
+    project(6, 9)
+    o_cp.wait()
     for g in range(DIM // 256):
         v4 = qkv[2 * PER + g // groups, :, pl.ds((g % groups) * 256, 256)]
         mixed = dot(probs[g], v4)
@@ -164,7 +167,6 @@
             c4 = jnp.where(lane_head == h, mixed[h * ROWS:(h + 1) * ROWS], c4)
         ctx[:, pl.ds(g * 256, 256)] = c4.astype(jnp.bfloat16)
 
-    o_cp.wait()
     h = (x_f + dot(ctx[...], wo_v[...])).astype(jnp.bfloat16)
     keep[...] = h.astype(jnp.float32)
     u_all[0] = rms_norm(h.astype(jnp.float32), mgain[...].astype(jnp.float32).reshape(1, DIM))
@@ -179,7 +181,8 @@
 
     d_cp = []
     for n in range(NBLK):
-        cp = pltpu.make_async_copy(wd.at[:, pl.ds(n * NB, NB)], buf1.at[:, pl.ds(n * NB, NB)], d_sem.at[n])
+        cols = pl.ds(NOFF[n], NBS[n])
+        cp = pltpu.make_async_copy(wd.at[:, cols], buf1.at[:, cols], d_sem.at[n])
         cp.start(priority=1)
         d_cp.append(cp)
 
@@ -234,65 +237,72 @@
                 hid[:, e] = (jax.nn.silu(gate_act) * up_act).astype(jnp.bfloat16).reshape(GROUP, 2 * SLOTS, FFN)
 
     relay(0)
+    gather(1, 0)
+    relay(1)
+    gather(1, 1)
     for k in range(len(KS)):
-        gather(1, k)
+        if k == 1:
+            relay(2)
+            gather(1, 2)
         u_copies[k][2].wait_recv()
         for cp in g_cp[k]:
             cp.wait()
         gather(3, k)
         half = LOCAL // 2
         experts(k, 0, half)
-        if k + 1 < len(KS):
-            relay(k + 1)
+        if k == 2:
+            relay(3)
+            gather(1, 3)
         experts(k, half, LOCAL)
 
-    sends = []
-    second = []
+    cols = [pl.ds(NOFF[n], NBS[n]) for n in range(NBLK)]
+    to_sib = [[remote(p_send.at[i, :, c], p_recv.at[i, :, c], ps_sem.at[n, i], pr_sem.at[n, i], sib) for i in range(2)] for n, c in enumerate(cols)]
+    to_cross = [remote(s_send.at[:, c], r_recv.at[:, c], ss_sem.at[n], rr_sem.at[n], cross) for n, c in enumerate(cols)]
 
     def forward(n):
-        sends[n][0].wait_recv()
-        s_send[n] = s_send[n] + p_recv[n, 1]
-        cp = remote(s_send.at[n], r_recv.at[n], ss_sem.at[n], rr_sem.at[n], cross)
-        cp.start()
-        second.append(cp)
+        to_sib[n][1].wait_recv()
+        s_send[:, cols[n]] = s_send[:, cols[n]] + p_recv[1, :, cols[n]]
+        to_cross[n].start()
 
     def down(n):
-        cols = pl.ds(n * NB, NB)
         for e in range(LOCAL):
-            res = dot(hid[:, e].reshape(EROWS, FFN), buf1[pl.ds(e * FFN, FFN), cols])
-            o_v[n % 2, :, e] = res.astype(jnp.bfloat16).reshape(GROUP, 2 * SLOTS, NB)
+            res = dot(hid[:, e].reshape(EROWS, FFN), buf1[pl.ds(e * FFN, FFN), cols[n]])
+            o_v[n % 2, :, e, :, pl.ds(0, NBS[n])] = res.astype(jnp.bfloat16).reshape(GROUP, 2 * SLOTS, NBS[n])
 
     def combine(n, r):
-        return dot(comb_t[r], o_v[n % 2, r].reshape(RROWS, NB))
+        return dot(comb_t[r], o_v[n % 2, r, :, :, pl.ds(0, NBS[n])].reshape(RROWS, NBS[n]))
 
     d_cp[0].wait()
     down(0)
+    p_send[1, :, cols[0]] = combine(0, 3)
+    to_sib[0][1].start()
     for n in range(NBLK):
         if n + 1 < NBLK:
             d_cp[n + 1].wait()
-        p_send[n, 1] = combine(n, 3)
-        p_send[n, 0] = combine(n, 2)
-        s_send[n] = combine(n, 1)
-        cols = pl.ds(n * NB, NB)
-        keep[:, cols] = keep[:, cols] + combine(n, 0)
+        if n > 0:
+            p_send[1, :, cols[n]] = combine(n, 3)
+        s_send[:, cols[n]] = combine(n, 1)
+        p_send[0, :, cols[n]] = combine(n, 2)
+        keep[:, cols[n]] = keep[:, cols[n]] + combine(n, 0)
         if n + 1 < NBLK:
             down(n + 1)
-        sends.append([remote(p_send.at[n, i], p_recv.at[n, i], ps_sem.at[n, i], pr_sem.at[n, i], sib) for i in (1, 0)])
-        for cp in sends[n]:
-            cp.start()
-        if n >= 1:
+        if n > 0:
+            to_sib[n][1].start()
+        to_sib[n][0].start()
+        if n > 1:
             forward(n - 1)
+        if n == 0:
+            forward(0)
     forward(NBLK - 1)
 
     for n in range(NBLK):
-        cols = pl.ds(n * NB, NB)
-        sends[n][1].wait_recv()
-        second[n].wait_recv()
-        out_v[:, cols] = (keep[:, cols] + p_recv[n, 0] + r_recv[n]).astype(jnp.bfloat16)
+        to_sib[n][0].wait_recv()
+        to_cross[n].wait_recv()
+        out_v[:, cols[n]] = (keep[:, cols[n]] + p_recv[0, :, cols[n]] + r_recv[:, cols[n]]).astype(jnp.bfloat16)
 
     out_cp = pltpu.make_async_copy(out_v, out_h, out_sem.at[0])
     out_cp.start()
-    for cp in (*c_copies, *g_copies, *(c for cs in u_copies for c in cs), *(c for cs in sends for c in cs), *second):
+    for cp in (*c_copies, *g_copies, *(c for cs in u_copies for c in cs), *(c for cs in to_sib for c in cs), *to_cross):
         cp.wait_send()
     out_cp.wait()
 
@@ -314,8 +324,8 @@
         pltpu.VMEM((NQ, ROWS, QCH), bf16), pltpu.VMEM((ROWS, DIM), bf16), pltpu.VMEM((GROUP, ROWS, DIM), bf16),
         pltpu.VMEM((GROUP, 2, TOP_K, SEQ), i32), pltpu.VMEM((GROUP, 2, TOP_K, SEQ), f32),
         pltpu.VMEM((GROUP, RROWS, ROWS), bf16), pltpu.VMEM((GROUP, ROWS, RROWS), bf16),
-        pltpu.VMEM((GROUP, LOCAL, 2 * SLOTS, DIM), bf16), pltpu.VMEM((GROUP, LOCAL, 2 * SLOTS, FFN), bf16), pltpu.VMEM((2, GROUP, LOCAL, 2 * SLOTS, NB), bf16),
-        pltpu.VMEM((NBLK, 2, ROWS, NB), f32), pltpu.VMEM((NBLK, 2, ROWS, NB), f32), pltpu.VMEM((NBLK, ROWS, NB), f32), pltpu.VMEM((NBLK, ROWS, NB), f32),
+        pltpu.VMEM((GROUP, LOCAL, 2 * SLOTS, DIM), bf16), pltpu.VMEM((GROUP, LOCAL, 2 * SLOTS, FFN), bf16), pltpu.VMEM((2, GROUP, LOCAL, 2 * SLOTS, max(NBS)), bf16),
+        pltpu.VMEM((2, ROWS, DIM), f32), pltpu.VMEM((2, ROWS, DIM), f32), pltpu.VMEM((ROWS, DIM), f32), pltpu.VMEM((ROWS, DIM), f32),
         pltpu.VMEM((ROWS, DIM), f32), pltpu.VMEM((ROWS, DIM), bf16), pltpu.VMEM((LOCAL, 2, EROWS, FFN), f32),
         dma((10,)), dma((NQ,)), dma((1,)), dma((2, len(KS))), dma((NBLK,)), dma((1,)),
         dma((2, 3)), dma((2, 3)), dma((len(KS), 3)), dma((len(KS), 3)), dma((NBLK, 2)), dma((NBLK, 2)), dma((NBLK,)), dma((NBLK,)),

time: 37.5 us -> 36.9 us (0.984)
  Pallas kernels: 36.7 us -> 36.1 us
    pallas_call x1, Pallas kernels: 35.1 us -> 34.5 us  [device_fn(): pl.pallas_call(layer_kernel, out_shape=jax.ShapeDtypeStruct((ROWS, DIM),...]
where the time goes in v4:
time: 36.9 us; the launch traced here: 36.7 us
  Pallas kernels  36.1 us (98%)
  between operations  0.65 us (2%)
    pallas_call x1, Pallas kernels, device_fn(): pl.pallas_call(layer_kernel, out_shape=jax.ShapeDtypeStruct((ROWS, DIM),...  34.5 us
    pallas_call x1, Pallas kernels, split(): pl.pallas_call(split_kernel, out_shape=(shape, shape), in_specs=[pl.Block...  1.62 us

profile of v4, /device:TPU:0, one launch (start us, length us, event | category | flops | bytes accessed | tf_op | source)
XLA Modules:
  0.0 36.7 jit_solution(13864984816982788185)
XLA Ops:
  0.6 34.5 %moe_layer.1.both = bf16[64,1536]{1,0:T(8,128)(2,1)} custom-call(bf16[32,1536]{1,0:T(8,128)(2,1)} %tok_a.1, s32[8,32]{1,0:T(8,128)} %bitcast.22, s32[8,32]{1,0:T(8,128)} %bitcast.23, bf16[8,32]{1,0:T(8,128)(2,1)} %bitcast.26, bf16[32,1536]{1,0:T(8,128)(2,1)} %tok_b.1, s32[8,32]{1,0:T(8,128)} %bitcast.24, s32[8,32]{1,0:T(8,128)} %bitcast.25, ...), custom_call_target="tpu_custom_call" | custom-call | tf_op jit(solution)/shard_map/moe_layer/pallas_call | solution.py:333
  35.1 1.6 %split.1 = (bf16[32,1536]{1,0:T(8,128)(2,1)}, bf16[32,1536]{1,0:T(8,128)(2,1)}) custom-call(bf16[64,1536]{1,0:T(8,128)(2,1)} %moe_layer.1.both), custom_call_target="tpu_custom_call" | custom-call | tf_op jit(solution)/shard_map/split/pallas_call | solution.py:355

commit v5 on v4

--- a/solution.py
+++ b/solution.py
@@ -10,7 +10,7 @@
 NORM_EPS = 1e-6
 MASK_VALUE = -1e30
 MESH = pl.DeviceIdType.MESH
-VMEM_LIMIT = 66_000_000
+VMEM_LIMIT = 53_000_000
 
 SEQ = 32
 ROWS = 2 * SEQ
@@ -27,13 +27,24 @@
 RROWS = LOCAL * 2 * SLOTS
 KS = (256, 256, 512, 512)
 KOFF = tuple(sum(KS[:k]) for k in range(len(KS)))
-NBS = (128, 256, 256, 256, 256, 256, 128)
+NBS = (256, 256, 256, 256, 256, 256)
 NOFF = tuple(sum(NBS[:n]) for n in range(len(NBS)))
 NBLK = len(NBS)
 QCH = 512
 PER = DIM // QCH
 NQ = 3 * PER
 
+BLK = 512
+PIECES = DIM // BLK
+X0, W0, Y0, Z0 = 0, 27, 36, 56
+POOL = 76
+KWHERE = ((Y0, 0), (Y0, 256), (Z0, 0), (X0, 0))
+DOWN = (
+    tuple(X0 + 20 + e for e in range(7)) + tuple(W0 + e for e in range(3)),
+    tuple(W0 + 3 + e for e in range(6)) + tuple(Y0 + e for e in range(4)),
+    tuple(Y0 + 4 + e for e in range(10)),
+)
+
 NT = (((1,), (1,)), ((), ()))
 NN = (((1,), (0,)), ((), ()))
 
@@ -50,9 +61,9 @@
 def layer_kernel(
     tok_a, exp_a, slot_a, gate_a, tok_b, exp_b, slot_b, gate_b, again_h, mgain_h, wq, wk, wv, wo, wg, wu, wd,
     out_h,
-    x_v, exp_v, slot_v, gate_v, again, mgain, buf1, wo_v, wg_v, wu_v, qkv, ctx, u_all, codes, gts, disp, comb_t, xg, hid, o_v,
-    p_send, p_recv, s_send, r_recv, keep, out_v, acc,
-    in_sem, q_sem, o_sem, g_sem, d_sem, out_sem, c_send, c_recv, u_send, u_recv, ps_sem, pr_sem, ss_sem, rr_sem,
+    x_v, exp_v, slot_v, gate_v, again, mgain, pool, qkv, ctx, u_all, codes, gts, disp, comb_t, xg, hid, o_v,
+    p_send, p_recv, s_send, r_recv, keep, acc,
+    in_sem, q_sem, o_sem, g_sem, d_sem, c_send, c_recv, u_send, u_recv, ps_sem, pr_sem, ss_sem, rr_sem,
 ):
     me = lax.axis_index("ep")
     dp = lax.axis_index("dp")
@@ -72,22 +83,34 @@
         ins.append(cp)
 
     q_cp = []
-    for i in range(NQ):
-        w, r = (wq, wk, wv)[i // PER], i % PER
-        cp = pltpu.make_async_copy(w.at[pl.ds(r * QCH, QCH)], buf1.at[pl.ds(i * QCH, QCH)], q_sem.at[i])
+    for i, (w, first, last) in enumerate(((wq, 0, 1), (wq, 1, 3), (wk, 0, 3), (wv, 0, 3))):
+        base = X0 + (0, 0, 3, 6)[i] + first
+        q_cp.append([
+            pltpu.make_async_copy(w.at[pl.ds(first, last - first), :, pl.ds(c * BLK, BLK)], pool.at[pl.ds(base + 9 * c, last - first)], q_sem.at[i, c])
+            for c in range(PIECES)
+        ])
+        for cp in q_cp[i]:
+            cp.start(priority=1)
+    o_cp = [pltpu.make_async_copy(wo.at[:, :, pl.ds(c * BLK, BLK)], pool.at[pl.ds(W0 + 3 * c, 3)], o_sem.at[c]) for c in range(PIECES)]
+    for cp in o_cp:
         cp.start(priority=1)
-        q_cp.append(cp)
-    o_cp = pltpu.make_async_copy(wo, wo_v, o_sem.at[0])
-    o_cp.start(priority=1)
 
     g_cp = []
     for k, (off, size) in enumerate(zip(KOFF, KS)):
-        ks = pl.ds(off, size)
-        g_cp.append([pltpu.make_async_copy(w.at[:, ks, :], v.at[:, ks, :], g_sem.at[i, k]) for i, (w, v) in enumerate(((wg, wg_v), (wu, wu_v)))])
+        base, row = KWHERE[k]
+        g_cp.append([
+            pltpu.make_async_copy(w.at[:, pl.ds(off, size), :], pool.at[pl.ds(base + LOCAL * i, LOCAL), pl.ds(row, size), :], g_sem.at[i, k])
+            for i, w in enumerate((wg, wu))
+        ])
 
     def fetch(k):
         for cp in g_cp[k]:
             cp.start(priority=1)
+
+    d_cp = []
+    for p, (first, last) in ((0, (0, 7)), (0, (7, 10)), (1, (0, 6)), (1, (6, 10)), (2, (0, 10))):
+        src = wd.at[pl.ds(first, last - first), :, pl.ds(p * BLK, BLK)]
+        d_cp.append(pltpu.make_async_copy(src, pool.at[pl.ds(DOWN[p][first], last - first)], d_sem.at[len(d_cp)]))
 
     barrier = pltpu.get_barrier_semaphore()
     for peer in (sib, cross):
@@ -114,21 +137,22 @@
     normed = rms_norm(x_f, again[...].astype(jnp.float32).reshape(1, DIM))
 
     def project(first, last):
-        rows = pl.ds(first * QCH, (last - first) * QCH)
-        res = dot(normed, buf1[rows, :], NT).astype(jnp.bfloat16)
         for i in range(first, last):
-            qkv[i] = res[:, (i - first) * QCH:(i - first + 1) * QCH]
-
-    q_cp[0].wait()
+            res = sum(dot(normed[:, c * BLK:(c + 1) * BLK], pool[X0 + 9 * c + i], NT) for c in range(PIECES))
+            qkv[i] = res.astype(jnp.bfloat16)
+
+    def arrived(copies):
+        for cp in copies:
+            cp.wait()
+
+    arrived(q_cp[0])
     fetch(0)
     project(0, 1)
-    q_cp[1].wait()
-    q_cp[2].wait()
+    arrived(q_cp[1])
     fetch(1)
     project(1, 3)
 
-    for i in (3, 4, 5):
-        q_cp[i].wait()
+    arrived(q_cp[2])
     fetch(2)
     project(3, 6)
 
@@ -138,9 +162,7 @@
     for cp in (*c_copies[:2], *g_copies[:2]):
         cp.start()
 
-    for i in (6, 7, 8):
-        q_cp[i].wait()
-    fetch(3)
+    arrived(q_cp[3])
     q_row = lax.rem(lax.broadcasted_iota(jnp.int32, (4 * ROWS, ROWS), 0), ROWS)
     k_col = lax.broadcasted_iota(jnp.int32, (4 * ROWS, ROWS), 1)
     seen = (k_col <= q_row) & (k_col // SEQ == q_row // SEQ)
@@ -158,7 +180,8 @@
         ex = jnp.exp(s - jnp.max(s, axis=-1, keepdims=True))
         probs.append((ex / jnp.sum(ex, axis=-1, keepdims=True)).astype(jnp.bfloat16))
     project(6, 9)
-    o_cp.wait()
+    fetch(3)
+    arrived(o_cp)
     for g in range(DIM // 256):
         v4 = qkv[2 * PER + g // groups, :, pl.ds((g % groups) * 256, 256)]
         mixed = dot(probs[g], v4)
@@ -167,7 +190,9 @@
             c4 = jnp.where(lane_head == h, mixed[h * ROWS:(h + 1) * ROWS], c4)
         ctx[:, pl.ds(g * 256, 256)] = c4.astype(jnp.bfloat16)
 
-    h = (x_f + dot(ctx[...], wo_v[...])).astype(jnp.bfloat16)
+    mixed_in = ctx[...]
+    attn_out = [sum(dot(mixed_in[:, i * BLK:(i + 1) * BLK], pool[W0 + 3 * c + i]) for i in range(3)) for c in range(PIECES)]
+    h = (x_f + jnp.concatenate(attn_out, axis=1)).astype(jnp.bfloat16)
     keep[...] = h.astype(jnp.float32)
     u_all[0] = rms_norm(h.astype(jnp.float32), mgain[...].astype(jnp.float32).reshape(1, DIM))
 
@@ -179,12 +204,8 @@
     for copies in u_copies:
         copies[1].start()
 
-    d_cp = []
-    for n in range(NBLK):
-        cols = pl.ds(NOFF[n], NBS[n])
-        cp = pltpu.make_async_copy(wd.at[:, cols], buf1.at[:, cols], d_sem.at[n])
+    for cp in d_cp[:3]:
         cp.start(priority=1)
-        d_cp.append(cp)
 
     c_copies[0].wait_recv()
     c_copies[2].start()
@@ -225,8 +246,10 @@
         ks = pl.ds(KOFF[k], KS[k])
         for e in range(first, last):
             xe = xg[:, e, :, ks].reshape(EROWS, KS[k])
-            gate_act = dot(xe, wg_v[e, ks, :])
-            up_act = dot(xe, wu_v[e, ks, :])
+            base, row = KWHERE[k]
+            rows = pl.ds(row, KS[k])
+            gate_act = dot(xe, pool[base + e, rows, :])
+            up_act = dot(xe, pool[base + LOCAL + e, rows, :])
             if k > 0:
                 gate_act = acc[e, 0] + gate_act
                 up_act = acc[e, 1] + up_act
@@ -254,6 +277,9 @@
             relay(3)
             gather(1, 3)
         experts(k, half, LOCAL)
+        if k == 1:
+            for cp in d_cp[3:]:
+                cp.start(priority=1)
 
     cols = [pl.ds(NOFF[n], NBS[n]) for n in range(NBLK)]
     to_sib = [[remote(p_send.at[i, :, c], p_recv.at[i, :, c], ps_sem.at[n, i], pr_sem.at[n, i], sib) for i in range(2)] for n, c in enumerate(cols)]
@@ -265,20 +291,23 @@
         to_cross[n].start()
 
     def down(n):
+        p, off = NOFF[n] // BLK, NOFF[n] % BLK
         for e in range(LOCAL):
-            res = dot(hid[:, e].reshape(EROWS, FFN), buf1[pl.ds(e * FFN, FFN), cols[n]])
+            res = dot(hid[:, e].reshape(EROWS, FFN), pool[DOWN[p][e], :, pl.ds(off, NBS[n])])
             o_v[n % 2, :, e, :, pl.ds(0, NBS[n])] = res.astype(jnp.bfloat16).reshape(GROUP, 2 * SLOTS, NBS[n])
 
     def combine(n, r):
         return dot(comb_t[r], o_v[n % 2, r, :, :, pl.ds(0, NBS[n])].reshape(RROWS, NBS[n]))
 
-    d_cp[0].wait()
+    arrived(d_cp[:2])
     down(0)
     p_send[1, :, cols[0]] = combine(0, 3)
     to_sib[0][1].start()
     for n in range(NBLK):
-        if n + 1 < NBLK:
-            d_cp[n + 1].wait()
+        if n + 1 < NBLK and NOFF[n + 1] == BLK:
+            arrived(d_cp[2:4])
+        if n + 1 < NBLK and NOFF[n + 1] == 2 * BLK:
+            arrived(d_cp[4:])
         if n > 0:
             p_send[1, :, cols[n]] = combine(n, 3)
         s_send[:, cols[n]] = combine(n, 1)
@@ -298,43 +327,41 @@
     for n in range(NBLK):
         to_sib[n][0].wait_recv()
         to_cross[n].wait_recv()
-        out_v[:, cols[n]] = (keep[:, cols[n]] + p_recv[0, :, cols[n]] + r_recv[:, cols[n]]).astype(jnp.bfloat16)
-
-    out_cp = pltpu.make_async_copy(out_v, out_h, out_sem.at[0])
-    out_cp.start()
+        out_h[:, cols[n]] = (keep[:, cols[n]] + p_recv[0, :, cols[n]] + r_recv[:, cols[n]]).astype(jnp.bfloat16)
+
     for cp in (*c_copies, *g_copies, *(c for cs in u_copies for c in cs), *(c for cs in to_sib for c in cs), *to_cross):
         cp.wait_send()
-    out_cp.wait()
 
 
 def device_fn(tokens_a, experts_a, slots_a, gates_a, tokens_b, experts_b, slots_b, gates_b, attn_gain, w_query, w_key, w_value, w_out, moe_gain, w_gate, w_up, w_down):
     def by_row(w):
-        return jnp.transpose(w, (1, 2, 0)).reshape(DIM, DIM)
+        return jnp.transpose(w, (1, 2, 0)).reshape(3, BLK, DIM)
 
     operands = (
         tokens_a, experts_a.T, slots_a.T, gates_a.T, tokens_b, experts_b.T, slots_b.T, gates_b.T, attn_gain, moe_gain,
-        by_row(w_query), by_row(w_key), by_row(w_value), w_out.reshape(DIM, DIM), w_gate, w_up, w_down.reshape(LOCAL * FFN, DIM),
+        by_row(w_query), by_row(w_key), by_row(w_value), w_out.reshape(3, BLK, DIM), w_gate, w_up, w_down,
     )
+    operands = tuple(pltpu.with_memory_space_constraint(x, pltpu.HBM) for x in operands)
     bf16, f32, i32 = jnp.bfloat16, jnp.float32, jnp.int32
     dma = pltpu.SemaphoreType.DMA
     scratch = [
         pltpu.VMEM((ROWS, DIM), bf16), pltpu.VMEM((2, TOP_K, SEQ), i32), pltpu.VMEM((2, TOP_K, SEQ), i32), pltpu.VMEM((2, TOP_K, SEQ), bf16),
         pltpu.VMEM((DIM,), bf16), pltpu.VMEM((DIM,), bf16),
-        pltpu.VMEM((LOCAL * FFN, DIM), bf16), pltpu.VMEM((DIM, DIM), bf16), pltpu.VMEM((LOCAL, DIM, FFN), bf16), pltpu.VMEM((LOCAL, DIM, FFN), bf16),
+        pltpu.VMEM((POOL, BLK, BLK), bf16),
         pltpu.VMEM((NQ, ROWS, QCH), bf16), pltpu.VMEM((ROWS, DIM), bf16), pltpu.VMEM((GROUP, ROWS, DIM), bf16),
         pltpu.VMEM((GROUP, 2, TOP_K, SEQ), i32), pltpu.VMEM((GROUP, 2, TOP_K, SEQ), f32),
         pltpu.VMEM((GROUP, RROWS, ROWS), bf16), pltpu.VMEM((GROUP, ROWS, RROWS), bf16),
         pltpu.VMEM((GROUP, LOCAL, 2 * SLOTS, DIM), bf16), pltpu.VMEM((GROUP, LOCAL, 2 * SLOTS, FFN), bf16), pltpu.VMEM((2, GROUP, LOCAL, 2 * SLOTS, max(NBS)), bf16),
         pltpu.VMEM((2, ROWS, DIM), f32), pltpu.VMEM((2, ROWS, DIM), f32), pltpu.VMEM((ROWS, DIM), f32), pltpu.VMEM((ROWS, DIM), f32),
-        pltpu.VMEM((ROWS, DIM), f32), pltpu.VMEM((ROWS, DIM), bf16), pltpu.VMEM((LOCAL, 2, EROWS, FFN), f32),
-        dma((10,)), dma((NQ,)), dma((1,)), dma((2, len(KS))), dma((NBLK,)), dma((1,)),
+        pltpu.VMEM((ROWS, DIM), f32), pltpu.VMEM((LOCAL, 2, EROWS, FFN), f32),
+        dma((10,)), dma((4, PIECES)), dma((PIECES,)), dma((2, len(KS))), dma((5,)),
         dma((2, 3)), dma((2, 3)), dma((len(KS), 3)), dma((len(KS), 3)), dma((NBLK, 2)), dma((NBLK, 2)), dma((NBLK,)), dma((NBLK,)),
     ]
     both = pl.pallas_call(
         layer_kernel,
         out_shape=jax.ShapeDtypeStruct((ROWS, DIM), bf16),
-        in_specs=[pl.BlockSpec(memory_space=pl.ANY)] * len(operands),
-        out_specs=pl.BlockSpec(memory_space=pl.ANY),
+        in_specs=[pl.BlockSpec(memory_space=pltpu.HBM)] * len(operands),
+        out_specs=pl.BlockSpec(memory_space=pltpu.VMEM),
         scratch_shapes=scratch,
         compiler_params=pltpu.CompilerParams(collective_id=0, has_side_effects=True, vmem_limit_bytes=VMEM_LIMIT),
         name="moe_layer",
@@ -355,9 +382,10 @@
     return pl.pallas_call(
         split_kernel,
         out_shape=(shape, shape),
-        in_specs=[pl.BlockSpec(memory_space=pltpu.VMEM)],
+        in_specs=[pl.BlockSpec(memory_space=pl.ANY)],
         out_specs=[pl.BlockSpec(memory_space=pl.ANY)] * 2,
         scratch_shapes=[pltpu.SemaphoreType.DMA((2,))],
+        compiler_params=pltpu.CompilerParams(vmem_limit_bytes=1 << 20),
         name="split",
     )(both)
 

time: 36.9 us -> 35.1 us (0.951)
  Pallas kernels: 36.1 us -> 34.3 us
    pallas_call x1, Pallas kernels: 1.62 us -> 0.69 us  [split(): pl.pallas_call(split_kernel, out_shape=(shape, shape), in_specs=[pl.Block...]
    pallas_call x1, Pallas kernels: 34.5 us -> 33.6 us  [device_fn(): pl.pallas_call(layer_kernel, out_shape=jax.ShapeDtypeStruct((ROWS, DIM),...]
where the time goes in v5:
time: 35.1 us; the launch traced here: 34.9 us
  Pallas kernels  34.3 us (98%)
  between operations  0.65 us (2%)
    pallas_call x1, Pallas kernels, device_fn(): pl.pallas_call(layer_kernel, out_shape=jax.ShapeDtypeStruct((ROWS, DIM),...  33.6 us

profile of v5, /device:TPU:0, one launch (start us, length us, event | category | flops | bytes accessed | tf_op | source)
XLA Modules:
  0.0 34.9 jit_solution(8933600489172886824)
XLA Ops:
  0.6 33.6 %moe_layer.1.both = bf16[64,1536]{1,0:T(8,128)(2,1)S(1)} custom-call(bf16[32,1536]{1,0:T(8,128)(2,1)} %tok_a.1, s32[8,32]{1,0:T(8,128)} %bitcast.20, s32[8,32]{1,0:T(8,128)} %bitcast.21, bf16[8,32]{1,0:T(8,128)(2,1)} %bitcast.24, bf16[32,1536]{1,0:T(8,128)(2,1)} %tok_b.1, s32[8,32]{1,0:T(8,128)} %bitcast.22, s32[8,32]{1,0:T(8,128)} %bitcast.23, ...), custom_call_target="tpu_custom_call" | custom-call | tf_op jit(solution)/shard_map/moe_layer/pallas_call | solution.py:360
  34.2 0.7 %split.1 = (bf16[32,1536]{1,0:T(8,128)(2,1)}, bf16[32,1536]{1,0:T(8,128)(2,1)}) custom-call(bf16[64,1536]{1,0:T(8,128)(2,1)S(1)} %moe_layer.1.both), custom_call_target="tpu_custom_call" | custom-call | tf_op jit(solution)/shard_map/split/pallas_call | solution.py:382

commit v6 on v5

--- a/solution.py
+++ b/solution.py
@@ -53,6 +53,11 @@
     return lax.dot_general(lhs, rhs, dims, preferred_element_type=jnp.float32)
 
 
+def dot_wide(lhs, rhs, dims=NN, copies=2):
+    rows = lhs.shape[0]
+    return dot(jnp.concatenate([lhs] * copies, axis=0), rhs, dims)[:rows]
+
+
 def rms_norm(rows_f, gain):
     inv_rms = lax.rsqrt(jnp.mean(rows_f * rows_f, axis=-1, keepdims=True) + NORM_EPS)
     return (rows_f * inv_rms * gain).astype(jnp.bfloat16)
@@ -98,19 +103,28 @@
     g_cp = []
     for k, (off, size) in enumerate(zip(KOFF, KS)):
         base, row = KWHERE[k]
-        g_cp.append([
-            pltpu.make_async_copy(w.at[:, pl.ds(off, size), :], pool.at[pl.ds(base + LOCAL * i, LOCAL), pl.ds(row, size), :], g_sem.at[i, k])
-            for i, w in enumerate((wg, wu))
-        ])
+        half = LOCAL // 2
+        for j in range(2):
+            g_cp.append([
+                pltpu.make_async_copy(
+                    w.at[pl.ds(j * half, half), pl.ds(off, size), :], pool.at[pl.ds(base + LOCAL * i + j * half, half), pl.ds(row, size), :], g_sem.at[i, 2 * k + j]
+                )
+                for i, w in enumerate((wg, wu))
+            ])
 
     def fetch(k):
-        for cp in g_cp[k]:
+        for cp in (*g_cp[2 * k], *g_cp[2 * k + 1]):
             cp.start(priority=1)
 
     d_cp = []
-    for p, (first, last) in ((0, (0, 7)), (0, (7, 10)), (1, (0, 6)), (1, (6, 10)), (2, (0, 10))):
-        src = wd.at[pl.ds(first, last - first), :, pl.ds(p * BLK, BLK)]
-        d_cp.append(pltpu.make_async_copy(src, pool.at[pl.ds(DOWN[p][first], last - first)], d_sem.at[len(d_cp)]))
+    half = BLK // 2
+    for p, (first, last), off, size in (
+        (0, (0, 7), 0, half), (0, (7, 10), 0, half), (0, (0, 7), half, half), (0, (7, 10), half, half),
+        (1, (0, 6), 0, BLK), (1, (6, 10), 0, BLK), (2, (0, 10), 0, BLK),
+    ):
+        src = wd.at[pl.ds(first, last - first), :, pl.ds(p * BLK + off, size)]
+        dst = pool.at[pl.ds(DOWN[p][first], last - first), :, pl.ds(off, size)]
+        d_cp.append(pltpu.make_async_copy(src, dst, d_sem.at[len(d_cp)]))
 
     barrier = pltpu.get_barrier_semaphore()
     for peer in (sib, cross):
@@ -138,7 +152,7 @@
 
     def project(first, last):
         for i in range(first, last):
-            res = sum(dot(normed[:, c * BLK:(c + 1) * BLK], pool[X0 + 9 * c + i], NT) for c in range(PIECES))
+            res = sum(dot_wide(normed[:, c * BLK:(c + 1) * BLK], pool[X0 + 9 * c + i], NT, 4) for c in range(PIECES))
             qkv[i] = res.astype(jnp.bfloat16)
 
     def arrived(copies):
@@ -191,7 +205,7 @@
         ctx[:, pl.ds(g * 256, 256)] = c4.astype(jnp.bfloat16)
 
     mixed_in = ctx[...]
-    attn_out = [sum(dot(mixed_in[:, i * BLK:(i + 1) * BLK], pool[W0 + 3 * c + i]) for i in range(3)) for c in range(PIECES)]
+    attn_out = [sum(dot_wide(mixed_in[:, i * BLK:(i + 1) * BLK], pool[W0 + 3 * c + i]) for i in range(3)) for c in range(PIECES)]
     h = (x_f + jnp.concatenate(attn_out, axis=1)).astype(jnp.bfloat16)
     keep[...] = h.astype(jnp.float32)
     u_all[0] = rms_norm(h.astype(jnp.float32), mgain[...].astype(jnp.float32).reshape(1, DIM))
@@ -204,7 +218,7 @@
     for copies in u_copies:
         copies[1].start()
 
-    for cp in d_cp[:3]:
+    for cp in d_cp[:5]:
         cp.start(priority=1)
 
     c_copies[0].wait_recv()
@@ -248,8 +262,8 @@
             xe = xg[:, e, :, ks].reshape(EROWS, KS[k])
             base, row = KWHERE[k]
             rows = pl.ds(row, KS[k])
-            gate_act = dot(xe, pool[base + e, rows, :])
-            up_act = dot(xe, pool[base + LOCAL + e, rows, :])
+            gate_act = dot_wide(xe, pool[base + e, rows, :])
+            up_act = dot_wide(xe, pool[base + LOCAL + e, rows, :])
             if k > 0:
                 gate_act = acc[e, 0] + gate_act
                 up_act = acc[e, 1] + up_act
@@ -268,17 +282,20 @@
             relay(2)
             gather(1, 2)
         u_copies[k][2].wait_recv()
-        for cp in g_cp[k]:
-            cp.wait()
+        arrived(g_cp[2 * k])
+        if k < 3:
+            arrived(g_cp[2 * k + 1])
         gather(3, k)
         half = LOCAL // 2
         experts(k, 0, half)
         if k == 2:
             relay(3)
             gather(1, 3)
+        if k == 3:
+            arrived(g_cp[2 * k + 1])
         experts(k, half, LOCAL)
         if k == 1:
-            for cp in d_cp[3:]:
+            for cp in d_cp[5:]:
                 cp.start(priority=1)
 
     cols = [pl.ds(NOFF[n], NBS[n]) for n in range(NBLK)]
@@ -293,7 +310,7 @@
     def down(n):
         p, off = NOFF[n] // BLK, NOFF[n] % BLK
         for e in range(LOCAL):
-            res = dot(hid[:, e].reshape(EROWS, FFN), pool[DOWN[p][e], :, pl.ds(off, NBS[n])])
+            res = dot_wide(hid[:, e].reshape(EROWS, FFN), pool[DOWN[p][e], :, pl.ds(off, NBS[n])])
             o_v[n % 2, :, e, :, pl.ds(0, NBS[n])] = res.astype(jnp.bfloat16).reshape(GROUP, 2 * SLOTS, NBS[n])
 
     def combine(n, r):
@@ -304,10 +321,12 @@
     p_send[1, :, cols[0]] = combine(0, 3)
     to_sib[0][1].start()
     for n in range(NBLK):
+        if n == 0:
+            arrived(d_cp[2:4])
         if n + 1 < NBLK and NOFF[n + 1] == BLK:
-            arrived(d_cp[2:4])
+            arrived(d_cp[4:6])
         if n + 1 < NBLK and NOFF[n + 1] == 2 * BLK:
-            arrived(d_cp[4:])
+            arrived(d_cp[6:])
         if n > 0:
             p_send[1, :, cols[n]] = combine(n, 3)
         s_send[:, cols[n]] = combine(n, 1)
@@ -354,7 +373,7 @@
         pltpu.VMEM((GROUP, LOCAL, 2 * SLOTS, DIM), bf16), pltpu.VMEM((GROUP, LOCAL, 2 * SLOTS, FFN), bf16), pltpu.VMEM((2, GROUP, LOCAL, 2 * SLOTS, max(NBS)), bf16),
         pltpu.VMEM((2, ROWS, DIM), f32), pltpu.VMEM((2, ROWS, DIM), f32), pltpu.VMEM((ROWS, DIM), f32), pltpu.VMEM((ROWS, DIM), f32),
         pltpu.VMEM((ROWS, DIM), f32), pltpu.VMEM((LOCAL, 2, EROWS, FFN), f32),
-        dma((10,)), dma((4, PIECES)), dma((PIECES,)), dma((2, len(KS))), dma((5,)),
+        dma((10,)), dma((4, PIECES)), dma((PIECES,)), dma((2, 2 * len(KS))), dma((7,)),
         dma((2, 3)), dma((2, 3)), dma((len(KS), 3)), dma((len(KS), 3)), dma((NBLK, 2)), dma((NBLK, 2)), dma((NBLK,)), dma((NBLK,)),
     ]
     both = pl.pallas_call(

time: 35.1 us -> 34.4 us (0.980)
  Pallas kernels: 34.3 us -> 33.6 us
    pallas_call x1, Pallas kernels: 33.6 us -> 32.9 us  [device_fn(): pl.pallas_call(layer_kernel, out_shape=jax.ShapeDtypeStruct((ROWS, DIM),...]
where the time goes in v6:
time: 34.4 us; the launch traced here: 34.2 us
  Pallas kernels  33.6 us (98%)
  between operations  0.65 us (2%)
    pallas_call x1, Pallas kernels, device_fn(): pl.pallas_call(layer_kernel, out_shape=jax.ShapeDtypeStruct((ROWS, DIM),...  32.9 us
    pallas_call x1, Pallas kernels, split(): pl.pallas_call(split_kernel, out_shape=(shape, shape), in_specs=[pl.Block...  0.69 us

profile of v6, /device:TPU:0, one launch (start us, length us, event | category | flops | bytes accessed | tf_op | source)
XLA Modules:
  0.0 34.2 jit_solution(16914050264058560478)
XLA Ops:
  0.6 32.9 %moe_layer.1.both = bf16[64,1536]{1,0:T(8,128)(2,1)S(1)} custom-call(bf16[32,1536]{1,0:T(8,128)(2,1)} %tok_a.1, s32[8,32]{1,0:T(8,128)} %bitcast.20, s32[8,32]{1,0:T(8,128)} %bitcast.21, bf16[8,32]{1,0:T(8,128)(2,1)} %bitcast.24, bf16[32,1536]{1,0:T(8,128)(2,1)} %tok_b.1, s32[8,32]{1,0:T(8,128)} %bitcast.22, s32[8,32]{1,0:T(8,128)} %bitcast.23, ...), custom_call_target="tpu_custom_call" | custom-call | tf_op jit(solution)/shard_map/moe_layer/pallas_call | solution.py:379
  33.6 0.7 %split.1 = (bf16[32,1536]{1,0:T(8,128)(2,1)}, bf16[32,1536]{1,0:T(8,128)(2,1)}) custom-call(bf16[64,1536]{1,0:T(8,128)(2,1)S(1)} %moe_layer.1.both), custom_call_target="tpu_custom_call" | custom-call | tf_op jit(solution)/shard_map/split/pallas_call | solution.py:401

commit v7 on v6

--- a/solution.py
+++ b/solution.py
@@ -38,6 +38,7 @@
 PIECES = DIM // BLK
 X0, W0, Y0, Z0 = 0, 27, 36, 56
 POOL = 76
+KPARTS = (((0, 10),), ((0, 10),), ((0, 5), (5, 10)), ((0, 5), (5, 8), (8, 10)))
 KWHERE = ((Y0, 0), (Y0, 256), (Z0, 0), (X0, 0))
 DOWN = (
     tuple(X0 + 20 + e for e in range(7)) + tuple(W0 + e for e in range(3)),
@@ -68,7 +69,7 @@
     out_h,
     x_v, exp_v, slot_v, gate_v, again, mgain, pool, qkv, ctx, u_all, codes, gts, disp, comb_t, xg, hid, o_v,
     p_send, p_recv, s_send, r_recv, keep, acc,
-    in_sem, q_sem, o_sem, g_sem, d_sem, c_send, c_recv, u_send, u_recv, ps_sem, pr_sem, ss_sem, rr_sem,
+    in_sem, q_sem, o_sem, g_sem, c_send, c_recv, u_send, u_recv, ps_sem, pr_sem, ss_sem, rr_sem,
 ):
     me = lax.axis_index("ep")
     dp = lax.axis_index("dp")
@@ -76,6 +77,7 @@
     core = lax.rem(me, 2)
     sib = (dp, x_pos * 2 + (1 - core))
     cross = (dp, (1 - x_pos) * 2 + core)
+    diag = (dp, (1 - x_pos) * 2 + (1 - core))
 
     ins = []
     for i, (src, dst) in enumerate([
@@ -100,21 +102,27 @@
     for cp in o_cp:
         cp.start(priority=1)
 
+    def part_sem(k, j, i):
+        if k < 2:
+            return g_sem.at[i, k]
+        at = 2 * j + i + (4 if k == 3 else 0)
+        return q_sem.at[at // PIECES, at % PIECES]
+
     g_cp = []
     for k, (off, size) in enumerate(zip(KOFF, KS)):
         base, row = KWHERE[k]
-        half = LOCAL // 2
-        for j in range(2):
-            g_cp.append([
-                pltpu.make_async_copy(
-                    w.at[pl.ds(j * half, half), pl.ds(off, size), :], pool.at[pl.ds(base + LOCAL * i + j * half, half), pl.ds(row, size), :], g_sem.at[i, 2 * k + j]
-                )
+        g_cp.append([])
+        for j, (first, last) in enumerate(KPARTS[k]):
+            ex = pl.ds(first, last - first)
+            g_cp[k].append([
+                pltpu.make_async_copy(w.at[ex, pl.ds(off, size), :], pool.at[pl.ds(base + LOCAL * i + first, last - first), pl.ds(row, size), :], part_sem(k, j, i))
                 for i, w in enumerate((wg, wu))
             ])
 
     def fetch(k):
-        for cp in (*g_cp[2 * k], *g_cp[2 * k + 1]):
-            cp.start(priority=1)
+        for part in g_cp[k]:
+            for cp in part:
+                cp.start(priority=1)
 
     d_cp = []
     half = BLK // 2
@@ -124,10 +132,10 @@
     ):
         src = wd.at[pl.ds(first, last - first), :, pl.ds(p * BLK + off, size)]
         dst = pool.at[pl.ds(DOWN[p][first], last - first), :, pl.ds(off, size)]
-        d_cp.append(pltpu.make_async_copy(src, dst, d_sem.at[len(d_cp)]))
+        d_cp.append(pltpu.make_async_copy(src, dst, in_sem.at[len(d_cp)]))
 
     barrier = pltpu.get_barrier_semaphore()
-    for peer in (sib, cross):
+    for peer in (sib, cross, diag):
         pl.semaphore_signal(barrier, inc=1, device_id=peer, device_id_type=MESH)
 
     for cp in ins:
@@ -143,9 +151,8 @@
 
     def exchange(buf, ssem, rsem):
         to_cross = remote(buf.at[0], buf.at[1], ssem.at[0], rsem.at[0], cross)
-        to_sib = remote(buf.at[0], buf.at[2], ssem.at[1], rsem.at[1], sib)
-        relay = remote(buf.at[1], buf.at[3], ssem.at[2], rsem.at[2], sib)
-        return to_cross, to_sib, relay
+        relay = remote(buf.at[1], buf.at[3], ssem.at[1], rsem.at[1], sib)
+        return to_cross, relay
 
     x_f = x_v[...].astype(jnp.float32)
     normed = rms_norm(x_f, again[...].astype(jnp.float32).reshape(1, DIM))
@@ -170,10 +177,12 @@
     fetch(2)
     project(3, 6)
 
-    pl.semaphore_wait(barrier, 2)
-    c_copies = exchange(codes, c_send.at[0], c_recv.at[0])
-    g_copies = exchange(gts, c_send.at[1], c_recv.at[1])
-    for cp in (*c_copies[:2], *g_copies[:2]):
+    pl.semaphore_wait(barrier, 3)
+    c_copies = [
+        remote(buf.at[0], buf.at[r], c_send.at[i, r - 1], c_recv.at[i, r - 1], dev)
+        for i, buf in enumerate((codes, gts)) for r, dev in ((1, cross), (2, sib), (3, diag))
+    ]
+    for cp in c_copies:
         cp.start()
 
     arrived(q_cp[3])
@@ -215,17 +224,13 @@
         view = u_all.at[:, :, pl.ds(off, size)]
         u_copies.append(exchange(view, u_send.at[k], u_recv.at[k]))
         u_copies[k][0].start()
-    for copies in u_copies:
-        copies[1].start()
+    u_sib = remote(u_all.at[0], u_all.at[2], u_send.at[len(KS), 0], u_recv.at[len(KS), 0], sib)
+    u_sib.start()
 
     for cp in d_cp[:5]:
         cp.start(priority=1)
 
-    c_copies[0].wait_recv()
-    c_copies[2].start()
-    g_copies[0].wait_recv()
-    g_copies[2].start()
-    for cp in (c_copies[1], g_copies[1], c_copies[2], g_copies[2]):
+    for cp in c_copies:
         cp.wait_recv()
     row = lax.broadcasted_iota(jnp.int32, (RROWS, ROWS), 0)
     want = (row // (2 * SLOTS) + me * LOCAL) * SLOTS + lax.rem(row, SLOTS) + lax.rem(row // SLOTS, 2) * (EXPERTS * SLOTS)
@@ -245,16 +250,9 @@
         ks = pl.ds(KOFF[k], KS[k])
         xg[r, :, :, ks] = dot(disp[r], u_all[r, :, ks]).astype(jnp.bfloat16).reshape(LOCAL, 2 * SLOTS, KS[k])
 
-    for k in range(len(KS)):
-        gather(0, k)
-    for k in range(len(KS)):
-        u_copies[k][1].wait_recv()
-    for k in range(len(KS)):
-        gather(2, k)
-
     def relay(k):
         u_copies[k][0].wait_recv()
-        u_copies[k][2].start()
+        u_copies[k][1].start()
 
     def experts(k, first, last):
         ks = pl.ds(KOFF[k], KS[k])
@@ -274,26 +272,32 @@
                 hid[:, e] = (jax.nn.silu(gate_act) * up_act).astype(jnp.bfloat16).reshape(GROUP, 2 * SLOTS, FFN)
 
     relay(0)
+    for k in range(len(KS)):
+        gather(0, k)
+    relay(1)
+    u_sib.wait_recv()
+    for k in range(len(KS)):
+        gather(2, k)
     gather(1, 0)
-    relay(1)
     gather(1, 1)
     for k in range(len(KS)):
         if k == 1:
             relay(2)
             gather(1, 2)
-        u_copies[k][2].wait_recv()
-        arrived(g_cp[2 * k])
-        if k < 3:
-            arrived(g_cp[2 * k + 1])
+        u_copies[k][1].wait_recv()
+        arrived(g_cp[k][0])
         gather(3, k)
-        half = LOCAL // 2
-        experts(k, 0, half)
         if k == 2:
+            experts(k, 0, 5)
             relay(3)
             gather(1, 3)
-        if k == 3:
-            arrived(g_cp[2 * k + 1])
-        experts(k, half, LOCAL)
+            arrived(g_cp[k][1])
+            experts(k, 5, LOCAL)
+        else:
+            for part, (first, last) in zip(g_cp[k], KPARTS[k]):
+                if first > 0:
+                    arrived(part)
+                experts(k, first, last)
         if k == 1:
             for cp in d_cp[5:]:
                 cp.start(priority=1)
@@ -348,7 +352,7 @@
         to_cross[n].wait_recv()
         out_h[:, cols[n]] = (keep[:, cols[n]] + p_recv[0, :, cols[n]] + r_recv[:, cols[n]]).astype(jnp.bfloat16)
 
-    for cp in (*c_copies, *g_copies, *(c for cs in u_copies for c in cs), *(c for cs in to_sib for c in cs), *to_cross):
+    for cp in (*c_copies, u_sib, *(c for cs in u_copies for c in cs), *(c for cs in to_sib for c in cs), *to_cross):
         cp.wait_send()
 
 
@@ -373,8 +377,8 @@
         pltpu.VMEM((GROUP, LOCAL, 2 * SLOTS, DIM), bf16), pltpu.VMEM((GROUP, LOCAL, 2 * SLOTS, FFN), bf16), pltpu.VMEM((2, GROUP, LOCAL, 2 * SLOTS, max(NBS)), bf16),
         pltpu.VMEM((2, ROWS, DIM), f32), pltpu.VMEM((2, ROWS, DIM), f32), pltpu.VMEM((ROWS, DIM), f32), pltpu.VMEM((ROWS, DIM), f32),
         pltpu.VMEM((ROWS, DIM), f32), pltpu.VMEM((LOCAL, 2, EROWS, FFN), f32),
-        dma((10,)), dma((4, PIECES)), dma((PIECES,)), dma((2, 2 * len(KS))), dma((7,)),
-        dma((2, 3)), dma((2, 3)), dma((len(KS), 3)), dma((len(KS), 3)), dma((NBLK, 2)), dma((NBLK, 2)), dma((NBLK,)), dma((NBLK,)),
+        dma((10,)), dma((4, PIECES)), dma((PIECES,)), dma((2, 2)),
+        dma((2, 3)), dma((2, 3)), dma((len(KS) + 1, 2)), dma((len(KS) + 1, 2)), dma((NBLK, 2)), dma((NBLK, 2)), dma((NBLK,)), dma((NBLK,)),
     ]
     both = pl.pallas_call(
         layer_kernel,

time: 34.4 us -> 34.2 us (level)
  no operation moved by 1% of the time
where the time goes in v7:
time: 34.2 us; the launch traced here: 34.1 us
  Pallas kernels  33.4 us (98%)
  between operations  0.65 us (2%)
    pallas_call x1, Pallas kernels, device_fn(): pl.pallas_call(layer_kernel, out_shape=jax.ShapeDtypeStruct((ROWS, DIM),...  32.7 us
    pallas_call x1, Pallas kernels, split(): pl.pallas_call(split_kernel, out_shape=(shape, shape), in_specs=[pl.Block...  0.69 us

profile of v7, /device:TPU:0, one launch (start us, length us, event | category | flops | bytes accessed | tf_op | source)
XLA Modules:
  0.0 34.1 jit_solution(11578577166635816652)
XLA Ops:
  0.6 32.7 %moe_layer.1.both = bf16[64,1536]{1,0:T(8,128)(2,1)S(1)} custom-call(bf16[32,1536]{1,0:T(8,128)(2,1)} %tok_a.1, s32[8,32]{1,0:T(8,128)} %bitcast.20, s32[8,32]{1,0:T(8,128)} %bitcast.21, bf16[8,32]{1,0:T(8,128)(2,1)} %bitcast.24, bf16[32,1536]{1,0:T(8,128)(2,1)} %tok_b.1, s32[8,32]{1,0:T(8,128)} %bitcast.22, s32[8,32]{1,0:T(8,128)} %bitcast.23, ...), custom_call_target="tpu_custom_call" | custom-call | tf_op jit(solution)/shard_map/moe_layer/pallas_call | solution.py:383
  33.4 0.7 %split.1 = (bf16[32,1536]{1,0:T(8,128)(2,1)}, bf16[32,1536]{1,0:T(8,128)(2,1)}) custom-call(bf16[64,1536]{1,0:T(8,128)(2,1)S(1)} %moe_layer.1.both), custom_call_target="tpu_custom_call" | custom-call | tf_op jit(solution)/shard_map/split/pallas_call | solution.py:405
